TPU v7x, 512 devices: a whole 4x8x8 slice. The times are simulated.
512 devices in a mesh: blk: 8 (over x, core), rows: 64 (over z, y).
Axes of the slice: x: 4, y: 8, z: 8, core: 2. Of those that a mesh axis runs over, the one named last changes fastest.
Arguments:
- snapshots: float32 [131072, 2048], P('rows', 'blk'), may hold values from -40 to 40
- grades: int32 [2048], P('blk'), may hold values from 0 to 7
- mover: int32 [3, 8], P(None, 'blk'), may hold values from 0 to 1
Outputs:
- basis: float32 [131072, 2048], P('rows', 'blk')
All inputs are finite; a program needn't handle non-finite values.
Results may differ from a plain program's by a relative error of at most 0.0001.
Values sent between devices are 32-bit elements; how exact they have to be, the bound alone decides.
No kernel may reach another device: no remote copies, remote signals or barrier semaphores. Data moves between devices by JAX's collectives and lax.ppermute only.
A program may use at most 64 MiB of HBM per device.

v0:
```python
import functools

import jax
import jax.numpy as jnp
from jax import lax
from jax.experimental import pallas as pl
from jax.experimental.pallas import tpu as pltpu
from jax.sharding import PartitionSpec as P

BW = 128
ROUNDS = 4
NS_STEPS = 3
ROW_TILE = 512
PARAMS = pltpu.CompilerParams(vmem_limit_bytes=16 * 2**20)

epsilon = 1e-06
relaxation = 1.2
EXACT = lax.Precision.HIGHEST
F32 = jnp.float32


def mm(a, b):
    return jnp.dot(a, b, precision=EXACT, preferred_element_type=F32)


def mm_t(a, b):
    dims = (((0,), (0,)), ((), ()))
    return lax.dot_general(a, b, dims, precision=EXACT, preferred_element_type=F32)


def in_two(value):
    high = value.astype(jnp.bfloat16)
    return high, (value - high.astype(F32)).astype(jnp.bfloat16)


def apply(left, right):
    left_high, left_low = in_two(left)
    right_high, right_low = in_two(right)
    dot = functools.partial(jnp.dot, preferred_element_type=F32)
    return dot(left_high, right_high) + (dot(left_high, right_low) + dot(left_low, right_high))


def add_product(left, right, out_ref):
    whole = mm_t(left, right)

    @pl.when(pl.program_id(0) == 0)
    def _():
        out_ref[...] = jnp.zeros_like(out_ref)

    out_ref[: 2 * BW, :] += whole[:, :BW]
    out_ref[2 * BW :, :] += whole[:, BW:]


def product_kernel(left_ref, right_ref, out_ref):
    add_product(left_ref[...], right_ref[...], out_ref)


def square_kernel(left_ref, out_ref):
    value = left_ref[...]
    add_product(value, value, out_ref)


def tiled(width=2 * BW):
    return pl.BlockSpec((ROW_TILE, width), lambda i: (i, 0))


def whole(rows):
    return pl.BlockSpec((rows, BW), lambda i: (0, 0))


def shape(rows, cols=BW):
    return jax.ShapeDtypeStruct((rows, cols), F32)


def product_halves(left, right=None):
    args = (left,) if right is None else (left, right)
    return pl.pallas_call(
        square_kernel if right is None else product_kernel,
        grid=(left.shape[0] // ROW_TILE,),
        in_specs=[tiled() for _ in args],
        out_specs=whole(4 * BW),
        out_shape=shape(4 * BW),
        compiler_params=PARAMS,
    )(*args)


def rotate_kernel(with_gram, pair_ref, prev_ref, stay_ref, sent_ref, out_ref, came_ref, gram_ref=None):
    came = apply(prev_ref[...], sent_ref[: 2 * BW, :])
    stays = apply(pair_ref[...], stay_ref[: 2 * BW, :])
    came_ref[...] = came
    out_ref[:, :BW] = stays
    out_ref[:, BW:] = came
    if with_gram:
        new = out_ref[...]
        add_product(new, new, gram_ref)


def rotate(pair, prev, stay, sent, with_gram):
    rows = pair.shape[0]
    return pl.pallas_call(
        functools.partial(rotate_kernel, with_gram),
        grid=(rows // ROW_TILE,),
        in_specs=[tiled(), tiled(), whole(stay.shape[0]), whole(sent.shape[0])],
        out_specs=[tiled(), tiled(BW)] + [whole(4 * BW)] * with_gram,
        out_shape=[shape(rows, 2 * BW), shape(rows)] + [shape(4 * BW)] * with_gram,
        compiler_params=PARAMS,
    )(pair, prev, stay, sent)


def join_kernel(prev_ref, cols_ref, passed_ref, out_ref):
    out_ref[:, :BW] = apply(prev_ref[...], cols_ref[: 2 * BW, :])
    out_ref[:, BW:] = passed_ref[...]


def join(prev, cols, passed):
    rows = prev.shape[0]
    return pl.pallas_call(
        join_kernel,
        grid=(rows // ROW_TILE,),
        in_specs=[tiled(), whole(cols.shape[0]), tiled(BW)],
        out_specs=tiled(),
        out_shape=shape(rows, 2 * BW),
        compiler_params=PARAMS,
    )(prev, cols, passed)


def last_kernel(pair_ref, left_ref, right_ref, out_ref):
    pair = pair_ref[...]
    cols = jnp.concatenate([left_ref[: 2 * BW, :], right_ref[: 2 * BW, :]], 1)
    out_ref[...] = apply(pair, cols)


def last(pair, left, right):
    rows = pair.shape[0]
    return pl.pallas_call(
        last_kernel,
        grid=(rows // ROW_TILE,),
        in_specs=[tiled(), whole(left.shape[0]), whole(right.shape[0])],
        out_specs=tiled(),
        out_shape=shape(rows, 2 * BW),
        compiler_params=PARAMS,
    )(pair, left, right)


def form(halves, cols):
    return mm(halves[: 2 * BW], cols[:BW]) + mm(halves[2 * BW :], cols[BW:])


def columns_kernel(late, *refs):
    row_of = lax.broadcasted_iota(jnp.int32, (BW, BW), 0)
    keep = row_of == lax.broadcasted_iota(jnp.int32, (BW, BW), 1)
    eye = jnp.where(keep, 1.0, 0.0).astype(F32)

    def upright(row):
        return jnp.sum(jnp.where(keep, row, 0.0), axis=1, keepdims=True)

    if late:
        gram_ref, stay_ref, sent_ref, rows_ref, move_out, stay_out = refs
        gram = gram_ref[...]
        cross = mm_t(stay_ref[: 2 * BW, :], form(gram, sent_ref[: 2 * BW, :]))
        squares_a = stay_ref[2 * BW : 2 * BW + 1, :]
        squares_b = sent_ref[2 * BW : 2 * BW + 1, :]
    else:
        gram_ref, rows_ref, move_out, stay_out = refs
        gram = gram_ref[...]
        cross = gram[2 * BW : 3 * BW]
        squares_a = jnp.sum(jnp.where(keep, gram[:BW], 0.0), axis=0, keepdims=True)
        squares_b = jnp.sum(jnp.where(keep, gram[3 * BW :], 0.0), axis=0, keepdims=True)
    labels_a, labels_b = rows_ref[0:1, :], rows_ref[1:2, :]
    sign, a_moves = rows_ref[2:3, :], rows_ref[3:4, :] > 0.5
    scale_a = upright(lax.rsqrt(squares_a + epsilon))
    scale_b = lax.rsqrt(squares_b + epsilon)
    gap = jnp.abs(upright(labels_a) - labels_b)
    scaled = cross * scale_a * scale_b / (1.0 + gap)
    total = jnp.sum(jnp.sum(scaled * scaled, axis=0, keepdims=True), axis=1, keepdims=True)
    gen = relaxation * scaled / jnp.sqrt(total + epsilon) * sign
    gen_t = gen.T
    factors = []
    corner = gen
    metrics = [eye + mm(gen, gen_t), eye + mm(gen_t, gen)]
    for sweep in range(NS_STEPS):
        steps = [1.5 * eye - 0.5 * metric for metric in metrics]
        factors = [mm(f, s) for f, s in zip(factors, steps)] if factors else steps
        corner = mm(corner, steps[1])
        if sweep + 1 < NS_STEPS:
            metrics = [mm(mm(m, s), s) for m, s in zip(metrics, steps)]
    corner_t = -corner.T
    row = lax.broadcasted_iota(jnp.int32, (8, BW), 0)
    for out_ref, pick in ((move_out, a_moves), (stay_out, jnp.logical_not(a_moves))):
        top = jnp.where(pick, factors[0], corner)
        bottom = jnp.where(pick, corner_t, factors[1])
        out_ref[:BW, :] = top
        out_ref[BW : 2 * BW, :] = bottom
        tail = jnp.where(row == 1, jnp.where(pick, labels_a, labels_b), 0.0)
        if not late:
            image = form(gram, jnp.concatenate([top, bottom], 0))
            squares = jnp.sum(top * image[:BW], axis=0, keepdims=True)
            squares += jnp.sum(bottom * image[BW:], axis=0, keepdims=True)
            tail = jnp.where(row == 0, jnp.maximum(squares, 0.0), tail)
        out_ref[2 * BW :, :] = tail


def columns(args, labels_a, labels_b, swapped, a_moves):
    sign = jnp.where(swapped, -1.0, 1.0)
    pick = jnp.where(a_moves, 1.0, 0.0)
    row = lax.broadcasted_iota(jnp.int32, (8, BW), 0)
    rows = jnp.where(row == 2, sign, pick)
    rows = jnp.where(row == 0, labels_a, jnp.where(row == 1, labels_b, rows))
    return pl.pallas_call(
        functools.partial(columns_kernel, len(args) > 1),
        out_shape=[shape(2 * BW + 8)] * 2,
        compiler_params=PARAMS,
    )(*args, rows)


def exchange_all(parts):
    return lax.all_to_all(parts, "rows", split_axis=0, concat_axis=0, tiled=True)


def to_next(value):
    peers = lax.axis_size("blk")
    return lax.ppermute(value, "blk", [(i, (i + 1) % peers) for i in range(peers)])


def body(snapshots, grades, mover):
    peers = lax.axis_size("rows")
    labels = grades.astype(F32)
    labels_a, labels_b = labels[None, :BW], labels[None, BW:]
    swapped = jnp.zeros((), bool)
    pair = snapshots
    prev = to_next(pair)
    product = product_halves(pair)
    for stage in range(ROUNDS // 2):
        early, late = 2 * stage, 2 * stage + 1
        part = exchange_all(product.reshape(peers, -1, BW)).sum(axis=0)
        product = product_halves(pair, prev)
        lines = product.reshape(peers, -1, BW)
        copies = jnp.broadcast_to(part, lines.shape)
        both = exchange_all(jnp.concatenate([copies, lines], 1))
        gram = both[:, : lines.shape[1]].reshape(product.shape)
        part = both[:, lines.shape[1] :].sum(axis=0)
        cross_gram = exchange_all(jnp.broadcast_to(part, lines.shape)).reshape(product.shape)
        first = mover[early, 0] == 0
        a_moves = first != swapped
        move, stay = columns((gram,), labels_a, labels_b, swapped, a_moves)
        labels_a = stay[2 * BW + 1 : 2 * BW + 2]
        swapped = first
        sent = to_next(move)
        labels_b = sent[2 * BW + 1 : 2 * BW + 2]
        pair_next, came = rotate(pair, prev, stay, sent, False)
        if late + 1 < ROUNDS:
            passed = to_next(came)
            prev_stay = to_next(stay)
            prev = join(prev, prev_stay, passed)
        pair = pair_next
        if late + 1 == ROUNDS:
            a_moves = jnp.logical_not(swapped)
        else:
            first = mover[late, 0] == 0
            a_moves = first != swapped
        move, stay = columns((cross_gram, stay, sent), labels_a, labels_b, swapped, a_moves)
        if late + 1 == ROUNDS:
            return last(pair, move, stay)
        labels_a = stay[2 * BW + 1 : 2 * BW + 2]
        swapped = first
        sent = to_next(move)
        labels_b = sent[2 * BW + 1 : 2 * BW + 2]
        prev_stay = to_next(stay)
        pair, came, product = rotate(pair, prev, stay, sent, True)
        passed = to_next(came)
        prev = join(prev, prev_stay, passed)


def solution(mesh):
    placed = (P("rows", "blk"), P("blk"), P(None, "blk"))
    return jax.shard_map(
        body, mesh=mesh, in_specs=placed, out_specs=P("rows", "blk"), check_vma=False
    )
```

profile of v0, /device:TPU:1, one launch (start us, length us, event | category | flops | bytes accessed | tf_op | source)
XLA Modules:
  0.0 203.2 jit_solution(13221379201657879056)
XLA Ops:
  4.2 3.0 %shard_map.37 = f32[512,128]{1,0:T(8,128)S(1)} custom-call(f32[2048,256]{1,0:T(8,128)S(1)} %copy-done), custom_call_target="tpu_custom_call" | custom-call | tf_op jit(solution)/shard_map/pallas_call | solution.py:77
  7.3 30.4 %all_to_all.30 = f32[64,8,128]{2,1,0:T(8,128)S(1)} all-to-all(f32[64,8,128]{2,1,0:T(8,128)S(1)} %bitcast.29), channel_id=1, replica_groups=mesh['blk'=8,'rows'=64] {'rows'}, dimensions={0} | all-to-all | bytes 524288 | tf_op jit(solution)/shard_map/all_to_all | solution.py:217
  37.8 4.4 %shard_map.38 = f32[512,128]{1,0:T(8,128)S(1)} custom-call(f32[2048,256]{1,0:T(8,128)S(1)} %copy-done.1, f32[2048,256]{1,0:T(8,128)} %collective-permute-done.right_ref.prev_ref), custom_call_target="tpu_custom_call" | custom-call | tf_op jit(solution)/shard_map/pallas_call | solution.py:77
  43.0 4.6 %all-to-all-start.1 = ((f32[64,16,128]{2,1,0:T(8,128)}), f32[64,16,128]{2,1,0:T(8,128)S(1)}, u32[]{:S(2)}, u32[]{:S(2)}) async-start(f32[64,16,128]{2,1,0:T(8,128)} %pad_maximum_fusion), calls=%async_computation.1 | async-start | bytes 1048576 | tf_op jit(solution)/shard_map/all_to_all | solution.py:217
  49.2 13.8 %all-to-all-done.1 = f32[64,16,128]{2,1,0:T(8,128)S(1)} async-done(((f32[64,16,128]{2,1,0:T(8,128)}), f32[64,16,128]{2,1,0:T(8,128)S(1)}, u32[]{:S(2)}, u32[]{:S(2)}) %all-to-all-start.1) | async-done | bytes 524320 | tf_op jit(solution)/shard_map/all_to_all | solution.py:217
  65.7 6.3 %collective-permute-start.1 = (f32[264,128]{1,0:T(8,128)S(1)}, f32[264,128]{1,0:T(8,128)S(1)}, u32[]{:S(2)}, u32[]{:S(2)}) collective-permute-start(f32[264,128]{1,0:T(8,128)S(1)} %get-tuple-element.20), channel_id=1, source_target_pairs={{0,64},{64,128},{128,192},{192,256},{256,320},{320,384},{384,448},... | collective-permute-start | bytes 405512 | tf_op jit(solution)/shard_map/ppermute | solution.py:222
  74.1 4.7 %shard_map.40 = (f32[2048,256]{1,0:T(8,128)S(1)}, f32[2048,128]{1,0:T(8,128)}) custom-call(f32[2048,256]{1,0:T(8,128)S(1)} %copy-done.1, f32[2048,256]{1,0:T(8,128)} %collective-permute-done.right_ref.prev_ref, f32[264,128]{1,0:T(8,128)S(1)} %get-tuple-element.19.stay_ref.refs_1_, f32[264,128]{1,0:T(8,128)S(1)} %collective-permute-done.1.sent_ref.refs_2_), custom_call_target="tpu_custom_call" | custom-call | tf_op jit(solution)/shard_map/pallas_call | solution.py:100
  83.9 4.8 %all-to-all-start.2 = ((f32[64,8,128]{2,1,0:T(8,128)}), f32[64,8,128]{2,1,0:T(8,128)S(1)}, u32[]{:S(2)}, u32[]{:S(2)}) async-start(f32[64,8,128]{2,1,0:T(8,128)} %broadcast_in_dim.103), calls=%async_computation.2 | async-start | bytes 524288 | tf_op jit(solution)/shard_map/all_to_all | solution.py:217
  89.1 13.0 %all-to-all-done.2 = f32[64,8,128]{2,1,0:T(8,128)S(1)} async-done(((f32[64,8,128]{2,1,0:T(8,128)}), f32[64,8,128]{2,1,0:T(8,128)S(1)}, u32[]{:S(2)}, u32[]{:S(2)}) %all-to-all-start.2) | async-done | bytes 262176 | tf_op jit(solution)/shard_map/all_to_all | solution.py:217
  102.1 2.7 %shard_map.42 = (f32[264,128]{1,0:T(8,128)S(1)}, f32[264,128]{1,0:T(8,128)S(1)}) custom-call(f32[512,128]{1,0:T(8,128)S(1)} %bitcast.31, f32[264,128]{1,0:T(8,128)S(1)} %get-tuple-element.19.stay_ref.refs_1_, f32[264,128]{1,0:T(8,128)S(1)} %collective-permute-done.1.sent_ref.refs_2_, f32[8,128]{1,0:T(8,128)S(1)} %select_select_fusion.2.refs_3_), custom_call_target="tpu_custom_call" | custom-call | tf_op jit(solution)/shard_map/pallas_call | solution.py:209
  107.0 3.3 %shard_map.41.prev_ref = f32[2048,256]{1,0:T(8,128)S(1)} custom-call(f32[2048,256]{1,0:T(8,128)} %collective-permute-done.right_ref.prev_ref, f32[264,128]{1,0:T(8,128)S(1)} %collective-permute-done.2.cols_ref, f32[2048,128]{1,0:T(8,128)S(1)} %collective-permute-done.3.passed_ref), custom_call_target="tpu_custom_call" | custom-call | tf_op jit(solution)/shard_map/pallas_call | solution.py:117
  110.4 8.5 %shard_map.43 = (f32[2048,256]{1,0:T(8,128)S(1)}, f32[2048,128]{1,0:T(8,128)S(1)}, f32[512,128]{1,0:T(8,128)}) custom-call(f32[2048,256]{1,0:T(8,128)S(1)} %copy-done.8, f32[2048,256]{1,0:T(8,128)S(1)} %shard_map.41.prev_ref, f32[264,128]{1,0:T(8,128)S(1)} %get-tuple-element.23.stay_ref, f32[264,128]{1,0:T(8,128)S(1)} %collective-permute-done.4.sent_ref), custom_call_target="tpu_custom_call" | custom-call | tf_op jit(solution)/shard_map/pallas_call | solution.py:100
  121.2 4.8 %all-to-all-start.3 = ((f32[64,8,128]{2,1,0:T(8,128)}), f32[64,8,128]{2,1,0:T(8,128)S(1)}, u32[]{:S(2)}, u32[]{:S(2)}) async-start(f32[64,8,128]{2,1,0:T(8,128)} %bitcast.9), calls=%async_computation.3 | async-start | bytes 524288 | tf_op jit(solution)/shard_map/all_to_all | solution.py:217
  126.6 12.0 %all-to-all-done.3 = f32[64,8,128]{2,1,0:T(8,128)S(1)} async-done(((f32[64,8,128]{2,1,0:T(8,128)}), f32[64,8,128]{2,1,0:T(8,128)S(1)}, u32[]{:S(2)}, u32[]{:S(2)}) %all-to-all-start.3) | async-done | bytes 262176 | tf_op jit(solution)/shard_map/all_to_all | solution.py:217
  141.8 3.0 %shard_map.45 = f32[512,128]{1,0:T(8,128)S(1)} custom-call(f32[2048,256]{1,0:T(8,128)S(1)} %copy-done.5, f32[2048,256]{1,0:T(8,128)S(1)} %shard_map.44.right_ref.prev_ref), custom_call_target="tpu_custom_call" | custom-call | tf_op jit(solution)/shard_map/pallas_call | solution.py:77
  145.6 5.7 %all-to-all-start.4 = ((f32[64,16,128]{2,1,0:T(8,128)}), f32[64,16,128]{2,1,0:T(8,128)S(1)}, u32[]{:S(2)}, u32[]{:S(2)}) async-start(f32[64,16,128]{2,1,0:T(8,128)} %pad_maximum_fusion.1), calls=%async_computation.4 | async-start | bytes 1048576 | tf_op jit(solution)/shard_map/all_to_all | solution.py:217
  152.2 14.9 %all-to-all-done.4 = f32[64,16,128]{2,1,0:T(8,128)S(1)} async-done(((f32[64,16,128]{2,1,0:T(8,128)}), f32[64,16,128]{2,1,0:T(8,128)S(1)}, u32[]{:S(2)}, u32[]{:S(2)}) %all-to-all-start.4) | async-done | bytes 524320 | tf_op jit(solution)/shard_map/all_to_all | solution.py:217
  167.1 2.7 %shard_map.46 = (f32[264,128]{1,0:T(8,128)S(1)}, f32[264,128]{1,0:T(8,128)S(1)}) custom-call(f32[512,128]{1,0:T(8,128)S(1)} %get-tuple-element.34.refs_0_, f32[8,128]{1,0:T(8,128)S(1)} %select_select_fusion.1.refs_1_), custom_call_target="tpu_custom_call" | custom-call | tf_op jit(solution)/shard_map/pallas_call | solution.py:209
  169.8 6.9 %collective-permute-start.7 = (f32[264,128]{1,0:T(8,128)S(1)}, f32[264,128]{1,0:T(8,128)S(1)}, u32[]{:S(2)}, u32[]{:S(2)}) collective-permute-start(f32[264,128]{1,0:T(8,128)S(1)} %get-tuple-element.29), channel_id=1, source_target_pairs={{0,64},{64,128},{128,192},{192,256},{256,320},{320,384},{384,448},... | collective-permute-start | bytes 405512 | tf_op jit(solution)/shard_map/ppermute | solution.py:222
  177.4 4.8 %all-to-all-start.5 = ((f32[64,8,128]{2,1,0:T(8,128)}), f32[64,8,128]{2,1,0:T(8,128)S(1)}, u32[]{:S(2)}, u32[]{:S(2)}) async-start(f32[64,8,128]{2,1,0:T(8,128)} %broadcast_in_dim.117), calls=%async_computation.5 | async-start | bytes 524288 | tf_op jit(solution)/shard_map/all_to_all | solution.py:217
  183.8 3.2 %shard_map.47 = (f32[2048,256]{1,0:T(8,128)S(1)}, f32[2048,128]{1,0:T(8,128)}) custom-call(f32[2048,256]{1,0:T(8,128)S(1)} %copy-done.6, f32[2048,256]{1,0:T(8,128)S(1)} %shard_map.44.right_ref.prev_ref, f32[264,128]{1,0:T(8,128)S(1)} %get-tuple-element.28.stay_ref.refs_1_, f32[264,128]{1,0:T(8,128)S(1)} %collective-permute-done.7.sent_ref.refs_2_), custom_call_target="tpu_custom_call" | custom-call | tf_op jit(solution)/shard_map/pallas_call | solution.py:100
  188.4 7.8 %all-to-all-done.5 = f32[64,8,128]{2,1,0:T(8,128)S(1)} async-done(((f32[64,8,128]{2,1,0:T(8,128)}), f32[64,8,128]{2,1,0:T(8,128)S(1)}, u32[]{:S(2)}, u32[]{:S(2)}) %all-to-all-start.5) | async-done | bytes 262176 | tf_op jit(solution)/shard_map/all_to_all | solution.py:217
  196.1 2.7 %shard_map.48 = (f32[264,128]{1,0:T(8,128)S(1)}, f32[264,128]{1,0:T(8,128)S(1)}) custom-call(f32[512,128]{1,0:T(8,128)S(1)} %bitcast.30, f32[264,128]{1,0:T(8,128)S(1)} %get-tuple-element.28.stay_ref.refs_1_, f32[264,128]{1,0:T(8,128)S(1)} %collective-permute-done.7.sent_ref.refs_2_, f32[8,128]{1,0:T(8,128)S(1)} %select_select_fusion.refs_3_), custom_call_target="tpu_custom_call" | custom-call | tf_op jit(solution)/shard_map/pallas_call | solution.py:209
  200.5 2.7 %shard_map.49 = f32[2048,256]{1,0:T(8,128)} custom-call(f32[2048,256]{1,0:T(8,128)S(1)} %copy-done.10, f32[264,128]{1,0:T(8,128)S(1)} %get-tuple-element.31.left_ref, f32[264,128]{1,0:T(8,128)S(1)} %get-tuple-element.32.right_ref), custom_call_target="tpu_custom_call" | custom-call | tf_op jit(solution)/shard_map/pallas_call | solution.py:135
  (78 shorter events, 30.0 us)
Async XLA Ops:
  0.0 37.8 %collective-permute-start = (f32[2048,256]{1,0:T(8,128)}, f32[2048,256]{1,0:T(8,128)}, u32[]{:S(2)}, u32[]{:S(2)}) collective-permute-start(f32[2048,256]{1,0:T(8,128)} %pair_ref.1), channel_id=1, source_target_pairs={{0,64},{64,128},{128,192},{192,256},{256,320},{320,384},{384,448},... | collective-permute-start | bytes 6291464 | tf_op jit(solution)/shard_map/ppermute | solution.py:222
  2.6 1.6 copy-start
  4.2 33.5 %copy-start.1 = (f32[2048,256]{1,0:T(8,128)S(1)}, f32[2048,256]{1,0:T(8,128)}, u32[]{:S(2)}) copy-start(f32[2048,256]{1,0:T(8,128)} %pair_ref.1) | copy-start | bytes 6291460
  42.1 5.5 %copy-start.16 = (s32[256]{0:T(256)S(1)}, s32[256]{0:T(256)}, u32[]{:S(2)}) copy-start(s32[256]{0:T(256)} %param.4) | copy-start | bytes 3076
  42.2 5.5 %copy-start.15 = (s32[3,1]{0,1:T(1,128)S(1)}, s32[3,1]{0,1:T(1,128)}, u32[]{:S(2)}) copy-start(s32[3,1]{0,1:T(1,128)} %param.5) | copy-start | bytes 40
  43.0 20.0 %all-to-all-start.1 = ((f32[64,16,128]{2,1,0:T(8,128)}), f32[64,16,128]{2,1,0:T(8,128)S(1)}, u32[]{:S(2)}, u32[]{:S(2)}) async-start(f32[64,16,128]{2,1,0:T(8,128)} %pad_maximum_fusion), calls=%async_computation.1 | async-start | bytes 1048576 | tf_op jit(solution)/shard_map/all_to_all | solution.py:217
  49.1 39.9 %copy-start.11 = (pred[8]{0:T(512)(128)(4,1)}, pred[8]{0:T(512)(128)(4,1)S(1)}, u32[]{:S(2)}) copy-start(pred[8]{0:T(512)(128)(4,1)S(1)} %get-tuple-element.42) | copy-start | bytes 28
  49.1 39.9 %copy-start.13 = (pred[8]{0:T(512)(128)(4,1)}, pred[8]{0:T(512)(128)(4,1)S(1)}, u32[]{:S(2)}) copy-start(pred[8]{0:T(512)(128)(4,1)S(1)} %get-tuple-element.43) | copy-start | bytes 28
  65.7 8.3 %collective-permute-start.1 = (f32[264,128]{1,0:T(8,128)S(1)}, f32[264,128]{1,0:T(8,128)S(1)}, u32[]{:S(2)}, u32[]{:S(2)}) collective-permute-start(f32[264,128]{1,0:T(8,128)S(1)} %get-tuple-element.20), channel_id=1, source_target_pairs={{0,64},{64,128},{128,192},{192,256},{256,320},{320,384},{384,448},... | collective-permute-start | bytes 405512 | tf_op jit(solution)/shard_map/ppermute | solution.py:222
  80.1 26.9 %collective-permute-start.3 = (f32[2048,128]{1,0:T(8,128)}, f32[2048,128]{1,0:T(8,128)S(1)}, u32[]{:S(2)}, u32[]{:S(2)}) collective-permute-start(f32[2048,128]{1,0:T(8,128)} %get-tuple-element.22), channel_id=1, source_target_pairs={{0,64},{64,128},{128,192},{192,256},{256,320},{320,384},{384,448},... | collective-permute-start | bytes 3145736 | tf_op jit(solution)/shard_map/ppermute | solution.py:222
  83.9 18.2 %all-to-all-start.2 = ((f32[64,8,128]{2,1,0:T(8,128)}), f32[64,8,128]{2,1,0:T(8,128)S(1)}, u32[]{:S(2)}, u32[]{:S(2)}) async-start(f32[64,8,128]{2,1,0:T(8,128)} %broadcast_in_dim.103), calls=%async_computation.2 | async-start | bytes 524288 | tf_op jit(solution)/shard_map/all_to_all | solution.py:217
  88.7 18.3 %collective-permute-start.2 = (f32[264,128]{1,0:T(8,128)S(1)}, f32[264,128]{1,0:T(8,128)S(1)}, u32[]{:S(2)}, u32[]{:S(2)}) collective-permute-start(f32[264,128]{1,0:T(8,128)S(1)} %get-tuple-element.19.stay_ref.refs_1_), channel_id=1, source_target_pairs={{0,64},{64,128},{128,192},{192,256},{256,320},{320,384},{384,448},... | collective-permute-start | bytes 405512 | tf_op jit(solution)/shard_map/ppermute | solution.py:222
  104.9 5.5 %copy-start.8 = (f32[2048,256]{1,0:T(8,128)S(1)}, f32[2048,256]{1,0:T(8,128)}, u32[]{:S(2)}) copy-start(f32[2048,256]{1,0:T(8,128)} %copy-done.7) | copy-start | bytes 6291460
  104.9 5.5 %collective-permute-start.4 = (f32[264,128]{1,0:T(8,128)S(1)}, f32[264,128]{1,0:T(8,128)S(1)}, u32[]{:S(2)}, u32[]{:S(2)}) collective-permute-start(f32[264,128]{1,0:T(8,128)S(1)} %get-tuple-element.24), channel_id=1, source_target_pairs={{0,64},{64,128},{128,192},{192,256},{256,320},{320,384},{384,448},... | collective-permute-start | bytes 405512 | tf_op jit(solution)/shard_map/ppermute | solution.py:222
  110.4 8.5 %copy-start.2 = (f32[2048,256]{1,0:T(8,128)}, f32[2048,256]{1,0:T(8,128)S(1)}, u32[]{:S(2)}) copy-start(f32[2048,256]{1,0:T(8,128)S(1)} %shard_map.41.prev_ref) | copy-start | bytes 6291460
  120.2 18.4 %collective-permute-start.6 = (f32[2048,128]{1,0:T(8,128)S(1)}, f32[2048,128]{1,0:T(8,128)S(1)}, u32[]{:S(2)}, u32[]{:S(2)}) collective-permute-start(f32[2048,128]{1,0:T(8,128)S(1)} %get-tuple-element.26), channel_id=1, source_target_pairs={{0,64},{64,128},{128,192},{192,256},{256,320},{320,384},{384,448},... | collective-permute-start | bytes 3145736 | tf_op jit(solution)/shard_map/ppermute | solution.py:222
  121.2 17.3 %all-to-all-start.3 = ((f32[64,8,128]{2,1,0:T(8,128)}), f32[64,8,128]{2,1,0:T(8,128)S(1)}, u32[]{:S(2)}, u32[]{:S(2)}) async-start(f32[64,8,128]{2,1,0:T(8,128)} %bitcast.9), calls=%async_computation.3 | async-start | bytes 524288 | tf_op jit(solution)/shard_map/all_to_all | solution.py:217
  126.0 12.6 %collective-permute-start.5 = (f32[264,128]{1,0:T(8,128)S(1)}, f32[264,128]{1,0:T(8,128)S(1)}, u32[]{:S(2)}, u32[]{:S(2)}) collective-permute-start(f32[264,128]{1,0:T(8,128)S(1)} %get-tuple-element.23.stay_ref), channel_id=1, source_target_pairs={{0,64},{64,128},{128,192},{192,256},{256,320},{320,384},{384,448},... | collective-permute-start | bytes 405512 | tf_op jit(solution)/shard_map/ppermute | solution.py:222
  144.8 7.3 %copy-start.12 = (pred[8]{0:T(512)(128)(4,1)S(1)}, pred[8]{0:T(512)(128)(4,1)}, u32[]{:S(2)}) copy-start(pred[8]{0:T(512)(128)(4,1)} %copy-done.11) | copy-start | bytes 28
  144.8 7.3 %copy-start.14 = (pred[8]{0:T(512)(128)(4,1)S(1)}, pred[8]{0:T(512)(128)(4,1)}, u32[]{:S(2)}) copy-start(pred[8]{0:T(512)(128)(4,1)} %copy-done.13) | copy-start | bytes 28
  145.6 21.4 %all-to-all-start.4 = ((f32[64,16,128]{2,1,0:T(8,128)}), f32[64,16,128]{2,1,0:T(8,128)S(1)}, u32[]{:S(2)}, u32[]{:S(2)}) async-start(f32[64,16,128]{2,1,0:T(8,128)} %pad_maximum_fusion.1), calls=%async_computation.4 | async-start | bytes 1048576 | tf_op jit(solution)/shard_map/all_to_all | solution.py:217
  169.8 12.4 %collective-permute-start.7 = (f32[264,128]{1,0:T(8,128)S(1)}, f32[264,128]{1,0:T(8,128)S(1)}, u32[]{:S(2)}, u32[]{:S(2)}) collective-permute-start(f32[264,128]{1,0:T(8,128)S(1)} %get-tuple-element.29), channel_id=1, source_target_pairs={{0,64},{64,128},{128,192},{192,256},{256,320},{320,384},{384,448},... | collective-permute-start | bytes 405512 | tf_op jit(solution)/shard_map/ppermute | solution.py:222
  177.4 18.8 %all-to-all-start.5 = ((f32[64,8,128]{2,1,0:T(8,128)}), f32[64,8,128]{2,1,0:T(8,128)S(1)}, u32[]{:S(2)}, u32[]{:S(2)}) async-start(f32[64,8,128]{2,1,0:T(8,128)} %broadcast_in_dim.117), calls=%async_computation.5 | async-start | bytes 524288 | tf_op jit(solution)/shard_map/all_to_all | solution.py:217
  182.2 1.6 copy-start.6
  (6 other events, 8.7 us)
where the time goes:
time: 204 us; the launch traced here: 203 us
  waiting for transfers between devices  63.5 us (31%)
  starting transfers between devices  47 us (23%)
  Pallas kernels  45.1 us (22%)
  blocking collectives  30.4 us (15%)
  local copies, waits for them, and re-layouts  12.5 us (6%)
  between operations  2.42 us (1%)
  other arithmetic  2.24 us (1%)
    all_to_all x5, waiting for transfers between devices, exchange_all(): lax.all_to_all(parts, 'rows', split_axis=0, concat_axis=0, tiled=True)  61.5 us
    all_to_all x1, blocking collectives, exchange_all(): lax.all_to_all(parts, 'rows', split_axis=0, concat_axis=0, tiled=True)  30.4 us
    all_to_all x5, starting transfers between devices, exchange_all(): lax.all_to_all(parts, 'rows', split_axis=0, concat_axis=0, tiled=True)  24.7 us
    ppermute x8, starting transfers between devices, to_next(): lax.ppermute(value, 'blk', [(i, (i + 1) % peers) for i in range(peers)])  22.3 us
    pallas_call x3, Pallas kernels, rotate(): pl.pallas_call(functools.partial(rotate_kernel, with_gram), grid=(rows //...  16.3 us
    pallas_call x4, Pallas kernels, columns(): pl.pallas_call(functools.partial(columns_kernel, len(args) > 1), out_shap...  10.8 us
    unnamed x34, local copies, waits for them, and re-layouts  10.4 us
    pallas_call x3, Pallas kernels, product_halves(): pl.pallas_call(square_kernel if right is None else product_kernel, grid=(...  10.4 us
  transfers between devices with their start and end apart: 13, of which 6 were waited for; matrix products, arithmetic and copies ran while one was open for 1% of the time, Pallas kernels for 6%

commit v1 on v0

--- a/solution.py
+++ b/solution.py
@@ -10,7 +10,7 @@
 BW = 128
 ROUNDS = 4
 NS_STEPS = 3
-ROW_TILE = 512
+ROW_TILE = 1024
 PARAMS = pltpu.CompilerParams(vmem_limit_bytes=16 * 2**20)
 
 epsilon = 1e-06
@@ -41,7 +41,16 @@
 
 
 def add_product(left, right, out_ref):
-    whole = mm_t(left, right)
+    dims = (((0,), (0,)), ((), ()))
+    dot_t = functools.partial(lax.dot_general, dimension_numbers=dims, preferred_element_type=F32)
+    left_high, left_low = in_two(left)
+    if right is None:
+        side = dot_t(left_high, left_low)
+        whole = dot_t(left_high, left_high) + (side + side.T)
+    else:
+        right_high, right_low = in_two(right)
+        cross = dot_t(left_high, right_low) + dot_t(left_low, right_high)
+        whole = dot_t(left_high, right_high) + cross
 
     @pl.when(pl.program_id(0) == 0)
     def _():
@@ -56,8 +65,7 @@
 
 
 def square_kernel(left_ref, out_ref):
-    value = left_ref[...]
-    add_product(value, value, out_ref)
+    add_product(left_ref[...], None, out_ref)
 
 
 def tiled(width=2 * BW):
@@ -72,7 +80,12 @@
     return jax.ShapeDtypeStruct((rows, cols), F32)
 
 
+def streamed(value):
+    return pltpu.with_memory_space_constraint(value, pltpu.HBM)
+
+
 def product_halves(left, right=None):
+    left = streamed(left)
     args = (left,) if right is None else (left, right)
     return pl.pallas_call(
         square_kernel if right is None else product_kernel,
@@ -84,25 +97,29 @@
     )(*args)
 
 
-def rotate_kernel(with_gram, pair_ref, prev_ref, stay_ref, sent_ref, out_ref, came_ref, gram_ref=None):
+def rotate_kernel(pair_ref, prev_ref, stay_ref, sent_ref, out_ref, came_ref=None, gram_ref=None):
     came = apply(prev_ref[...], sent_ref[: 2 * BW, :])
     stays = apply(pair_ref[...], stay_ref[: 2 * BW, :])
-    came_ref[...] = came
     out_ref[:, :BW] = stays
     out_ref[:, BW:] = came
+    if gram_ref is not None:
+        came_ref[...] = came
+        add_product(jnp.concatenate([stays, came], 1), None, gram_ref)
+
+
+def rotate(pair, prev, stay, sent, with_gram=False):
+    rows = pair.shape[0]
+    pair = streamed(pair)
     if with_gram:
-        new = out_ref[...]
-        add_product(new, new, gram_ref)
-
-
-def rotate(pair, prev, stay, sent, with_gram):
-    rows = pair.shape[0]
-    return pl.pallas_call(
-        functools.partial(rotate_kernel, with_gram),
+        prev = streamed(prev)
+    out_specs = (tiled(), tiled(BW), whole(4 * BW))
+    out_shape = (pltpu.HBM((rows, 2 * BW), F32), shape(rows), shape(4 * BW))
+    return pl.pallas_call(
+        rotate_kernel,
         grid=(rows // ROW_TILE,),
         in_specs=[tiled(), tiled(), whole(stay.shape[0]), whole(sent.shape[0])],
-        out_specs=[tiled(), tiled(BW)] + [whole(4 * BW)] * with_gram,
-        out_shape=[shape(rows, 2 * BW), shape(rows)] + [shape(4 * BW)] * with_gram,
+        out_specs=out_specs if with_gram else out_specs[0],
+        out_shape=out_shape if with_gram else out_shape[0],
         compiler_params=PARAMS,
     )(pair, prev, stay, sent)
 
@@ -112,16 +129,24 @@
     out_ref[:, BW:] = passed_ref[...]
 
 
-def join(prev, cols, passed):
+def join_two_kernel(prev_ref, cols_ref, other_ref, other_cols_ref, out_ref):
+    out_ref[:, :BW] = apply(prev_ref[...], cols_ref[: 2 * BW, :])
+    out_ref[:, BW:] = apply(other_ref[...], other_cols_ref[: 2 * BW, :])
+
+
+def join(prev, cols, passed, passed_cols=None):
     rows = prev.shape[0]
-    return pl.pallas_call(
-        join_kernel,
+    if passed_cols is None:
+        prev = streamed(prev)
+    args = (prev, cols, passed) if passed_cols is None else (prev, cols, passed, passed_cols)
+    return pl.pallas_call(
+        join_kernel if passed_cols is None else join_two_kernel,
         grid=(rows // ROW_TILE,),
-        in_specs=[tiled(), whole(cols.shape[0]), tiled(BW)],
+        in_specs=[tiled(a.shape[1]) if a.shape[0] == rows else whole(a.shape[0]) for a in args],
         out_specs=tiled(),
-        out_shape=shape(rows, 2 * BW),
-        compiler_params=PARAMS,
-    )(prev, cols, passed)
+        out_shape=shape(rows, 2 * BW) if passed_cols is None else pltpu.HBM((rows, 2 * BW), F32),
+        compiler_params=PARAMS,
+    )(*args)
 
 
 def last_kernel(pair_ref, left_ref, right_ref, out_ref):
@@ -131,6 +156,7 @@
 
 
 def last(pair, left, right):
+    pair = streamed(pair)
     rows = pair.shape[0]
     return pl.pallas_call(
         last_kernel,
@@ -214,7 +240,8 @@
 
 
 def exchange_all(parts):
-    return lax.all_to_all(parts, "rows", split_axis=0, concat_axis=0, tiled=True)
+    flat = parts.reshape(parts.shape[0], 1, -1)
+    return lax.all_to_all(flat, "rows", split_axis=0, concat_axis=0, tiled=True).reshape(parts.shape)
 
 
 def to_next(value):
@@ -236,6 +263,8 @@
         product = product_halves(pair, prev)
         lines = product.reshape(peers, -1, BW)
         copies = jnp.broadcast_to(part, lines.shape)
+        if late + 1 < ROUNDS:
+            before = to_next(prev)
         both = exchange_all(jnp.concatenate([copies, lines], 1))
         gram = both[:, : lines.shape[1]].reshape(product.shape)
         part = both[:, lines.shape[1] :].sum(axis=0)
@@ -247,12 +276,11 @@
         swapped = first
         sent = to_next(move)
         labels_b = sent[2 * BW + 1 : 2 * BW + 2]
-        pair_next, came = rotate(pair, prev, stay, sent, False)
+        pair = rotate(pair, prev, stay, sent)
         if late + 1 < ROUNDS:
-            passed = to_next(came)
             prev_stay = to_next(stay)
-            prev = join(prev, prev_stay, passed)
-        pair = pair_next
+            sent_before = to_next(sent)
+            prev = join(prev, prev_stay, before, sent_before)
         if late + 1 == ROUNDS:
             a_moves = jnp.logical_not(swapped)
         else:

time: 204 us -> 191 us (0.936)
  blocking collectives: 30.4 us -> 0 us
  waiting for transfers between devices: 63.5 us -> 79 us
  starting transfers between devices: 47 us -> 61.1 us
  local copies, waits for them, and re-layouts: 12.5 us -> 2.38 us
  Pallas kernels: 45.1 us -> 42.9 us
    all_to_all x1 -> x0, blocking collectives: 30.4 us -> none  [exchange_all(): lax.all_to_all(parts, 'rows', split_axis=0, concat_axis=0, tiled=True)]
    all_to_all x5 -> x6, starting transfers between devices: 24.7 us -> 45.2 us  [exchange_all(): lax.all_to_all(flat, 'rows', split_axis=0, concat_axis=0, tiled=True)]
    all_to_all x5 -> x6, waiting for transfers between devices: 61.5 us -> 75.2 us  [exchange_all(): lax.all_to_all(flat, 'rows', split_axis=0, concat_axis=0, tiled=True)]
    unnamed x34 -> x12, local copies, waits for them, and re-layouts: 10.4 us -> 0.03 us
    ppermute x8 -> x9, starting transfers between devices: 22.3 us -> 15.9 us  [to_next(): lax.ppermute(value, 'blk', [(i, (i + 1) % peers) for i in range(peers)])]
    pallas_call x3, Pallas kernels: 10.4 us -> 8.25 us  [product_halves(): pl.pallas_call(square_kernel if right is None else product_kernel, grid=(...]
  transfers between devices with their start and end apart: 13 -> 15, of which waited for: 6 -> 7; matrix products, arithmetic and copies ran while one was open for 1% -> 2% of each run, Pallas kernels for 6% -> 12%
where the time goes in v1:
time: 191 us; the launch traced here: 190 us
  waiting for transfers between devices  79 us (41%)
  starting transfers between devices  61.1 us (32%)
  Pallas kernels  42.9 us (22%)
  other arithmetic  2.48 us (1%)
  local copies, waits for them, and re-layouts  2.38 us (1%)
  between operations  2.16 us (1%)
    all_to_all x6, waiting for transfers between devices, exchange_all(): lax.all_to_all(flat, 'rows', split_axis=0, concat_axis=0, tiled=True)  75.2 us
    all_to_all x6, starting transfers between devices, exchange_all(): lax.all_to_all(flat, 'rows', split_axis=0, concat_axis=0, tiled=True)  45.2 us
    ppermute x9, starting transfers between devices, to_next(): lax.ppermute(value, 'blk', [(i, (i + 1) % peers) for i in range(peers)])  15.9 us
    pallas_call x3, Pallas kernels, rotate(): pl.pallas_call(rotate_kernel, grid=(rows // ROW_TILE,), in_specs=[tiled()...  13.8 us
    pallas_call x4, Pallas kernels, columns(): pl.pallas_call(functools.partial(columns_kernel, len(args) > 1), out_shap...  10.8 us
    pallas_call x3, Pallas kernels, product_halves(): pl.pallas_call(square_kernel if right is None else product_kernel, grid=(...  8.25 us
    pallas_call x2, Pallas kernels, join(): pl.pallas_call(join_kernel if passed_cols is None else join_two_kernel, g...  6.73 us
    ppermute x9, waiting for transfers between devices, to_next(): lax.ppermute(value, 'blk', [(i, (i + 1) % peers) for i in range(peers)])  3.89 us
  transfers between devices with their start and end apart: 15, of which 7 were waited for; matrix products, arithmetic and copies ran while one was open for 2% of the time, Pallas kernels for 12%

profile of v1, /device:TPU:1, one launch (start us, length us, event | category | flops | bytes accessed | tf_op | source)
XLA Modules:
  0.0 190.1 jit_solution(11078811946029128819)
XLA Ops:
  2.6 3.1 %shard_map.37 = f32[512,128]{1,0:T(8,128)} custom-call(f32[2048,256]{1,0:T(8,128)} %pair_ref.1), custom_call_target="tpu_custom_call" | custom-call | tf_op jit(solution)/shard_map/pallas_call | solution.py:90
  5.7 16.3 %all-to-all-start = ((f32[64,1,1024]{2,1,0:T(1,128)}), f32[64,1,1024]{2,1,0:T(1,128)S(1)}, u32[]{:S(2)}, u32[]{:S(2)}) async-start(f32[64,1,1024]{2,1,0:T(1,128)} %bitcast), calls=%async_computation | async-start | bytes 524288 | tf_op jit(solution)/shard_map/all_to_all | solution.py:244
  22.0 3.9 %collective-permute-done.right_ref.prev_ref = f32[2048,256]{1,0:T(8,128)S(1)} collective-permute-done((f32[2048,256]{1,0:T(8,128)}, f32[2048,256]{1,0:T(8,128)S(1)}, u32[]{:S(2)}, u32[]{:S(2)}) %collective-permute-start) | collective-permute-done | bytes 2097184 | tf_op jit(solution)/shard_map/ppermute | solution.py:249
  28.3 8.1 %all-to-all-done = f32[64,1,1024]{2,1,0:T(1,128)S(1)} async-done(((f32[64,1,1024]{2,1,0:T(1,128)}), f32[64,1,1024]{2,1,0:T(1,128)S(1)}, u32[]{:S(2)}, u32[]{:S(2)}) %all-to-all-start) | async-done | bytes 262176 | tf_op jit(solution)/shard_map/all_to_all | solution.py:244
  40.0 8.2 %all-to-all-start.1 = ((f32[64,1,2048]{2,1,0:T(1,128)}), f32[64,1,2048]{2,1,0:T(1,128)S(1)}, u32[]{:S(2)}, u32[]{:S(2)}) async-start(f32[64,1,2048]{2,1,0:T(1,128)} %bitcast.3), calls=%async_computation.1 | async-start | bytes 1048576 | tf_op jit(solution)/shard_map/all_to_all | solution.py:244
  50.3 15.8 %all-to-all-done.1 = f32[64,1,2048]{2,1,0:T(1,128)S(1)} async-done(((f32[64,1,2048]{2,1,0:T(1,128)}), f32[64,1,2048]{2,1,0:T(1,128)S(1)}, u32[]{:S(2)}, u32[]{:S(2)}) %all-to-all-start.1) | async-done | bytes 524320 | tf_op jit(solution)/shard_map/all_to_all | solution.py:244
  66.2 2.7 %shard_map.39 = (f32[264,128]{1,0:T(8,128)S(1)}, f32[264,128]{1,0:T(8,128)S(1)}) custom-call(f32[512,128]{1,0:T(8,128)S(1)} %get-tuple-element.30.refs_0_, f32[8,128]{1,0:T(8,128)S(1)} %select_select_fusion.3.refs_1_), custom_call_target="tpu_custom_call" | custom-call | tf_op jit(solution)/shard_map/pallas_call | solution.py:235
  71.3 6.4 %all-to-all-start.2 = ((f32[64,1,1024]{2,1,0:T(1,128)}), f32[64,1,1024]{2,1,0:T(1,128)S(1)}, u32[]{:S(2)}, u32[]{:S(2)}) async-start(f32[64,1,1024]{2,1,0:T(1,128)} %broadcast_in_dim.108), calls=%async_computation.2 | async-start | bytes 524288 | tf_op jit(solution)/shard_map/all_to_all | solution.py:244
  79.8 12.1 %all-to-all-done.2 = f32[64,1,1024]{2,1,0:T(1,128)S(1)} async-done(((f32[64,1,1024]{2,1,0:T(1,128)}), f32[64,1,1024]{2,1,0:T(1,128)S(1)}, u32[]{:S(2)}, u32[]{:S(2)}) %all-to-all-start.2) | async-done | bytes 262176 | tf_op jit(solution)/shard_map/all_to_all | solution.py:244
  91.9 2.7 %shard_map.42 = (f32[264,128]{1,0:T(8,128)S(1)}, f32[264,128]{1,0:T(8,128)S(1)}) custom-call(f32[512,128]{1,0:T(8,128)S(1)} %bitcast.37, f32[264,128]{1,0:T(8,128)S(1)} %get-tuple-element.16.stay_ref.refs_1_, f32[264,128]{1,0:T(8,128)S(1)} %collective-permute-done.1.sent_ref.refs_2_, f32[8,128]{1,0:T(8,128)S(1)} %select_select_fusion.2.refs_3_), custom_call_target="tpu_custom_call" | custom-call | tf_op jit(solution)/shard_map/pallas_call | solution.py:235
  95.7 4.2 %shard_map.40.pair_ref = f32[2048,256]{1,0:T(8,128)} custom-call(f32[2048,256]{1,0:T(8,128)} %pair_ref.1, f32[2048,256]{1,0:T(8,128)S(1)} %collective-permute-done.right_ref.prev_ref, f32[264,128]{1,0:T(8,128)S(1)} %get-tuple-element.16.stay_ref.refs_1_, f32[264,128]{1,0:T(8,128)S(1)} %collective-permute-done.1.sent_ref.refs_2_), custom_call_target="tpu_custom_call" | custom-call | tf_op jit(solution)/shard_map/pallas_call | solution.py:117
  99.9 4.2 %shard_map.41.prev_ref = f32[2048,256]{1,0:T(8,128)} custom-call(f32[2048,256]{1,0:T(8,128)S(1)} %collective-permute-done.right_ref.prev_ref, f32[264,128]{1,0:T(8,128)S(1)} %collective-permute-done.2.cols_ref, f32[2048,256]{1,0:T(8,128)} %collective-permute-done.3.other_ref, f32[264,128]{1,0:T(8,128)S(1)} %collective-permute-done.4.other_cols_ref), custom_call_target="tpu_custom_call" | custom-call | tf_op jit(solution)/shard_map/pallas_call | solution.py:142
  104.1 5.4 %shard_map.43 = (f32[2048,256]{1,0:T(8,128)}, f32[2048,128]{1,0:T(8,128)S(1)}, f32[512,128]{1,0:T(8,128)}) custom-call(f32[2048,256]{1,0:T(8,128)} %shard_map.40.pair_ref, f32[2048,256]{1,0:T(8,128)} %shard_map.41.prev_ref, f32[264,128]{1,0:T(8,128)S(1)} %get-tuple-element.18.stay_ref, f32[264,128]{1,0:T(8,128)S(1)} %collective-permute-done.5.sent_ref), custom_call_target="tpu_custom_call" | custom-call | tf_op jit(solution)/shard_map/pallas_call | solution.py:117
  110.7 4.8 %all-to-all-start.3 = ((f32[64,1,1024]{2,1,0:T(1,128)}), f32[64,1,1024]{2,1,0:T(1,128)S(1)}, u32[]{:S(2)}, u32[]{:S(2)}) async-start(f32[64,1,1024]{2,1,0:T(1,128)} %bitcast.13), calls=%async_computation.3 | async-start | bytes 524288 | tf_op jit(solution)/shard_map/all_to_all | solution.py:244
  116.8 12.8 %all-to-all-done.3 = f32[64,1,1024]{2,1,0:T(1,128)S(1)} async-done(((f32[64,1,1024]{2,1,0:T(1,128)}), f32[64,1,1024]{2,1,0:T(1,128)S(1)}, u32[]{:S(2)}, u32[]{:S(2)}) %all-to-all-start.3) | async-done | bytes 262176 | tf_op jit(solution)/shard_map/all_to_all | solution.py:244
  135.8 4.8 %all-to-all-start.4 = ((f32[64,1,2048]{2,1,0:T(1,128)}), f32[64,1,2048]{2,1,0:T(1,128)S(1)}, u32[]{:S(2)}, u32[]{:S(2)}) async-start(f32[64,1,2048]{2,1,0:T(1,128)} %bitcast.16), calls=%async_computation.4 | async-start | bytes 1048576 | tf_op jit(solution)/shard_map/all_to_all | solution.py:244
  141.3 16.6 %all-to-all-done.4 = f32[64,1,2048]{2,1,0:T(1,128)S(1)} async-done(((f32[64,1,2048]{2,1,0:T(1,128)}), f32[64,1,2048]{2,1,0:T(1,128)S(1)}, u32[]{:S(2)}, u32[]{:S(2)}) %all-to-all-start.4) | async-done | bytes 524320 | tf_op jit(solution)/shard_map/all_to_all | solution.py:244
  158.0 2.7 %shard_map.46 = (f32[264,128]{1,0:T(8,128)S(1)}, f32[264,128]{1,0:T(8,128)S(1)}) custom-call(f32[512,128]{1,0:T(8,128)S(1)} %get-tuple-element.28.refs_0_, f32[8,128]{1,0:T(8,128)S(1)} %select_select_fusion.1.refs_1_), custom_call_target="tpu_custom_call" | custom-call | tf_op jit(solution)/shard_map/pallas_call | solution.py:235
  160.7 3.8 %collective-permute-start.8 = (f32[264,128]{1,0:T(8,128)S(1)}, f32[264,128]{1,0:T(8,128)S(1)}, u32[]{:S(2)}, u32[]{:S(2)}) collective-permute-start(f32[264,128]{1,0:T(8,128)S(1)} %get-tuple-element.24), channel_id=1, source_target_pairs={{0,64},{64,128},{128,192},{192,256},{256,320},{320,384},{384,448},... | collective-permute-start | bytes 405512 | tf_op jit(solution)/shard_map/ppermute | solution.py:249
  165.3 4.7 %all-to-all-start.5 = ((f32[64,1,1024]{2,1,0:T(1,128)}), f32[64,1,1024]{2,1,0:T(1,128)S(1)}, u32[]{:S(2)}, u32[]{:S(2)}) async-start(f32[64,1,1024]{2,1,0:T(1,128)} %broadcast_in_dim.123), calls=%async_computation.5 | async-start | bytes 524288 | tf_op jit(solution)/shard_map/all_to_all | solution.py:244
  170.0 4.2 %shard_map.47.pair_ref = f32[2048,256]{1,0:T(8,128)} custom-call(f32[2048,256]{1,0:T(8,128)} %get-tuple-element.20.left_ref.pair_ref, f32[2048,256]{1,0:T(8,128)S(1)} %shard_map.44.right_ref.prev_ref, f32[264,128]{1,0:T(8,128)S(1)} %get-tuple-element.23.stay_ref.refs_1_, f32[264,128]{1,0:T(8,128)S(1)} %collective-permute-done.8.sent_ref.refs_2_), custom_call_target="tpu_custom_call" | custom-call | tf_op jit(solution)/shard_map/pallas_call | solution.py:117
  174.3 9.7 %all-to-all-done.5 = f32[64,1,1024]{2,1,0:T(1,128)S(1)} async-done(((f32[64,1,1024]{2,1,0:T(1,128)}), f32[64,1,1024]{2,1,0:T(1,128)S(1)}, u32[]{:S(2)}, u32[]{:S(2)}) %all-to-all-start.5) | async-done | bytes 262176 | tf_op jit(solution)/shard_map/all_to_all | solution.py:244
  184.0 2.7 %shard_map.48 = (f32[264,128]{1,0:T(8,128)S(1)}, f32[264,128]{1,0:T(8,128)S(1)}) custom-call(f32[512,128]{1,0:T(8,128)S(1)} %bitcast.38, f32[264,128]{1,0:T(8,128)S(1)} %get-tuple-element.23.stay_ref.refs_1_, f32[264,128]{1,0:T(8,128)S(1)} %collective-permute-done.8.sent_ref.refs_2_, f32[8,128]{1,0:T(8,128)S(1)} %select_select_fusion.refs_3_), custom_call_target="tpu_custom_call" | custom-call | tf_op jit(solution)/shard_map/pallas_call | solution.py:235
  186.7 3.4 %shard_map.49 = f32[2048,256]{1,0:T(8,128)} custom-call(f32[2048,256]{1,0:T(8,128)} %shard_map.47.pair_ref, f32[264,128]{1,0:T(8,128)S(1)} %get-tuple-element.25.left_ref, f32[264,128]{1,0:T(8,128)S(1)} %get-tuple-element.26.right_ref), custom_call_target="tpu_custom_call" | custom-call | tf_op jit(solution)/shard_map/pallas_call | solution.py:161
  (59 shorter events, 24.6 us)
Async XLA Ops:
  0.0 25.9 %collective-permute-start = (f32[2048,256]{1,0:T(8,128)}, f32[2048,256]{1,0:T(8,128)S(1)}, u32[]{:S(2)}, u32[]{:S(2)}) collective-permute-start(f32[2048,256]{1,0:T(8,128)} %pair_ref.1), channel_id=1, source_target_pairs={{0,64},{64,128},{128,192},{192,256},{256,320},{320,384},{384,448},... | collective-permute-start | bytes 6291464 | tf_op jit(solution)/shard_map/ppermute | solution.py:249
  5.7 30.6 %all-to-all-start = ((f32[64,1,1024]{2,1,0:T(1,128)}), f32[64,1,1024]{2,1,0:T(1,128)S(1)}, u32[]{:S(2)}, u32[]{:S(2)}) async-start(f32[64,1,1024]{2,1,0:T(1,128)} %bitcast), calls=%async_computation | async-start | bytes 524288 | tf_op jit(solution)/shard_map/all_to_all | solution.py:244
  25.9 74.0 %collective-permute-start.3 = (f32[2048,256]{1,0:T(8,128)S(1)}, f32[2048,256]{1,0:T(8,128)}, u32[]{:S(2)}, u32[]{:S(2)}) collective-permute-start(f32[2048,256]{1,0:T(8,128)S(1)} %collective-permute-done.right_ref.prev_ref), channel_id=1, source_target_pairs={{0,64},{64,128},{128,192},{192,256},{256,320},{320,384},{384,448},... | collective-permute-start | bytes 6291464 | tf_op jit(solution)/shard_map/ppermute | solution.py:249
  39.1 9.1 %copy-start.5 = (s32[256]{0:T(256)S(1)}, s32[256]{0:T(256)}, u32[]{:S(2)}) copy-start(s32[256]{0:T(256)} %param.4) | copy-start | bytes 3076
  39.1 9.1 %copy-start.4 = (s32[3,1]{0,1:T(1,128)S(1)}, s32[3,1]{0,1:T(1,128)}, u32[]{:S(2)}) copy-start(s32[3,1]{0,1:T(1,128)} %param.5) | copy-start | bytes 40
  40.0 26.1 %all-to-all-start.1 = ((f32[64,1,2048]{2,1,0:T(1,128)}), f32[64,1,2048]{2,1,0:T(1,128)S(1)}, u32[]{:S(2)}, u32[]{:S(2)}) async-start(f32[64,1,2048]{2,1,0:T(1,128)} %bitcast.3), calls=%async_computation.1 | async-start | bytes 1048576 | tf_op jit(solution)/shard_map/all_to_all | solution.py:244
  50.2 41.7 %copy-start = (pred[8]{0:T(512)(128)(4,1)}, pred[8]{0:T(512)(128)(4,1)S(1)}, u32[]{:S(2)}) copy-start(pred[8]{0:T(512)(128)(4,1)S(1)} %get-tuple-element.36) | copy-start | bytes 28
  50.2 41.7 %copy-start.2 = (pred[8]{0:T(512)(128)(4,1)}, pred[8]{0:T(512)(128)(4,1)S(1)}, u32[]{:S(2)}) copy-start(pred[8]{0:T(512)(128)(4,1)S(1)} %get-tuple-element.37) | copy-start | bytes 28
  68.8 9.3 %collective-permute-start.1 = (f32[264,128]{1,0:T(8,128)S(1)}, f32[264,128]{1,0:T(8,128)S(1)}, u32[]{:S(2)}, u32[]{:S(2)}) collective-permute-start(f32[264,128]{1,0:T(8,128)S(1)} %get-tuple-element.17), channel_id=1, source_target_pairs={{0,64},{64,128},{128,192},{192,256},{256,320},{320,384},{384,448},... | collective-permute-start | bytes 405512 | tf_op jit(solution)/shard_map/ppermute | solution.py:249
  71.3 20.6 %all-to-all-start.2 = ((f32[64,1,1024]{2,1,0:T(1,128)}), f32[64,1,1024]{2,1,0:T(1,128)S(1)}, u32[]{:S(2)}, u32[]{:S(2)}) async-start(f32[64,1,1024]{2,1,0:T(1,128)} %broadcast_in_dim.108), calls=%async_computation.2 | async-start | bytes 524288 | tf_op jit(solution)/shard_map/all_to_all | solution.py:244
  77.8 22.1 %collective-permute-start.2 = (f32[264,128]{1,0:T(8,128)S(1)}, f32[264,128]{1,0:T(8,128)S(1)}, u32[]{:S(2)}, u32[]{:S(2)}) collective-permute-start(f32[264,128]{1,0:T(8,128)S(1)} %get-tuple-element.16.stay_ref.refs_1_), channel_id=1, source_target_pairs={{0,64},{64,128},{128,192},{192,256},{256,320},{320,384},{384,448},... | collective-permute-start | bytes 405512 | tf_op jit(solution)/shard_map/ppermute | solution.py:249
  78.2 21.7 %collective-permute-start.4 = (f32[264,128]{1,0:T(8,128)S(1)}, f32[264,128]{1,0:T(8,128)S(1)}, u32[]{:S(2)}, u32[]{:S(2)}) collective-permute-start(f32[264,128]{1,0:T(8,128)S(1)} %collective-permute-done.1.sent_ref.refs_2_), channel_id=1, source_target_pairs={{0,64},{64,128},{128,192},{192,256},{256,320},{320,384},{384,448},... | collective-permute-start | bytes 405512 | tf_op jit(solution)/shard_map/ppermute | solution.py:249
  94.6 9.5 %collective-permute-start.5 = (f32[264,128]{1,0:T(8,128)S(1)}, f32[264,128]{1,0:T(8,128)S(1)}, u32[]{:S(2)}, u32[]{:S(2)}) collective-permute-start(f32[264,128]{1,0:T(8,128)S(1)} %get-tuple-element.19), channel_id=1, source_target_pairs={{0,64},{64,128},{128,192},{192,256},{256,320},{320,384},{384,448},... | collective-permute-start | bytes 405512 | tf_op jit(solution)/shard_map/ppermute | solution.py:249
  109.5 20.3 %collective-permute-start.7 = (f32[2048,128]{1,0:T(8,128)S(1)}, f32[2048,128]{1,0:T(8,128)S(1)}, u32[]{:S(2)}, u32[]{:S(2)}) collective-permute-start(f32[2048,128]{1,0:T(8,128)S(1)} %get-tuple-element.21), channel_id=1, source_target_pairs={{0,64},{64,128},{128,192},{192,256},{256,320},{320,384},{384,448},... | collective-permute-start | bytes 3145736 | tf_op jit(solution)/shard_map/ppermute | solution.py:249
  110.7 18.9 %all-to-all-start.3 = ((f32[64,1,1024]{2,1,0:T(1,128)}), f32[64,1,1024]{2,1,0:T(1,128)S(1)}, u32[]{:S(2)}, u32[]{:S(2)}) async-start(f32[64,1,1024]{2,1,0:T(1,128)} %bitcast.13), calls=%async_computation.3 | async-start | bytes 524288 | tf_op jit(solution)/shard_map/all_to_all | solution.py:244
  115.6 14.3 %collective-permute-start.6 = (f32[264,128]{1,0:T(8,128)S(1)}, f32[264,128]{1,0:T(8,128)S(1)}, u32[]{:S(2)}, u32[]{:S(2)}) collective-permute-start(f32[264,128]{1,0:T(8,128)S(1)} %get-tuple-element.18.stay_ref), channel_id=1, source_target_pairs={{0,64},{64,128},{128,192},{192,256},{256,320},{320,384},{384,448},... | collective-permute-start | bytes 405512 | tf_op jit(solution)/shard_map/ppermute | solution.py:249
  134.9 6.3 %copy-start.1 = (pred[8]{0:T(512)(128)(4,1)S(1)}, pred[8]{0:T(512)(128)(4,1)}, u32[]{:S(2)}) copy-start(pred[8]{0:T(512)(128)(4,1)} %copy-done) | copy-start | bytes 28
  134.9 6.3 %copy-start.3 = (pred[8]{0:T(512)(128)(4,1)S(1)}, pred[8]{0:T(512)(128)(4,1)}, u32[]{:S(2)}) copy-start(pred[8]{0:T(512)(128)(4,1)} %copy-done.2) | copy-start | bytes 28
  135.8 22.1 %all-to-all-start.4 = ((f32[64,1,2048]{2,1,0:T(1,128)}), f32[64,1,2048]{2,1,0:T(1,128)S(1)}, u32[]{:S(2)}, u32[]{:S(2)}) async-start(f32[64,1,2048]{2,1,0:T(1,128)} %bitcast.16), calls=%async_computation.4 | async-start | bytes 1048576 | tf_op jit(solution)/shard_map/all_to_all | solution.py:244
  160.7 9.3 %collective-permute-start.8 = (f32[264,128]{1,0:T(8,128)S(1)}, f32[264,128]{1,0:T(8,128)S(1)}, u32[]{:S(2)}, u32[]{:S(2)}) collective-permute-start(f32[264,128]{1,0:T(8,128)S(1)} %get-tuple-element.24), channel_id=1, source_target_pairs={{0,64},{64,128},{128,192},{192,256},{256,320},{320,384},{384,448},... | collective-permute-start | bytes 405512 | tf_op jit(solution)/shard_map/ppermute | solution.py:249
  165.3 18.7 %all-to-all-start.5 = ((f32[64,1,1024]{2,1,0:T(1,128)}), f32[64,1,1024]{2,1,0:T(1,128)S(1)}, u32[]{:S(2)}, u32[]{:S(2)}) async-start(f32[64,1,1024]{2,1,0:T(1,128)} %broadcast_in_dim.123), calls=%async_computation.5 | async-start | bytes 524288 | tf_op jit(solution)/shard_map/all_to_all | solution.py:244

commit v2 on v1

--- a/solution.py
+++ b/solution.py
@@ -11,6 +11,7 @@
 ROUNDS = 4
 NS_STEPS = 3
 ROW_TILE = 1024
+PACKED = 5 * 64
 PARAMS = pltpu.CompilerParams(vmem_limit_bytes=16 * 2**20)
 
 epsilon = 1e-06
@@ -40,32 +41,69 @@
     return dot(left_high, right_high) + (dot(left_high, right_low) + dot(left_low, right_high))
 
 
-def add_product(left, right, out_ref):
+def transposed_dot(left, right):
     dims = (((0,), (0,)), ((), ()))
-    dot_t = functools.partial(lax.dot_general, dimension_numbers=dims, preferred_element_type=F32)
-    left_high, left_low = in_two(left)
-    if right is None:
-        side = dot_t(left_high, left_low)
-        whole = dot_t(left_high, left_high) + (side + side.T)
-    else:
-        right_high, right_low = in_two(right)
-        cross = dot_t(left_high, right_low) + dot_t(left_low, right_high)
-        whole = dot_t(left_high, right_high) + cross
+    return lax.dot_general(left, right, dims, preferred_element_type=F32)
+
+
+def unit():
+    row = lax.broadcasted_iota(jnp.int32, (BW, BW), 0)
+    return row, lax.broadcasted_iota(jnp.int32, (BW, BW), 1)
+
+
+def product_kernel(left_ref, right_ref, out_ref):
+    left_high, left_low = in_two(left_ref[...])
+    right_high, right_low = in_two(right_ref[...])
+    cross = transposed_dot(left_high, right_low) + transposed_dot(left_low, right_high)
+    value = transposed_dot(left_high, right_high) + cross
 
     @pl.when(pl.program_id(0) == 0)
     def _():
         out_ref[...] = jnp.zeros_like(out_ref)
 
-    out_ref[: 2 * BW, :] += whole[:, :BW]
-    out_ref[2 * BW :, :] += whole[:, BW:]
-
-
-def product_kernel(left_ref, right_ref, out_ref):
-    add_product(left_ref[...], right_ref[...], out_ref)
-
-
-def square_kernel(left_ref, out_ref):
-    add_product(left_ref[...], None, out_ref)
+    out_ref[: 2 * BW, :] += value[:, :BW]
+    out_ref[2 * BW :, :] += value[:, BW:]
+
+
+def add_square(value, total_ref, out_ref):
+    high, low = in_two(value)
+    side = transposed_dot(high, low)
+    value = transposed_dot(high, high) + (side + side.T)
+    step = pl.program_id(0)
+
+    @pl.when(step == 0)
+    def _():
+        total_ref[...] = value
+
+    @pl.when(step > 0)
+    def _():
+        total_ref[...] += value
+
+    @pl.when(step == pl.num_programs(0) - 1)
+    def _():
+        row, col = unit()
+        second = total_ref[BW:, BW:]
+        out_ref[:BW, :] = total_ref[:BW, BW:]
+        out_ref[BW : 2 * BW, :] = jnp.where(row <= col, total_ref[:BW, :BW], second)
+        ends = jnp.sum(jnp.where(row == col, second, 0.0), axis=0, keepdims=True)
+        out_ref[2 * BW :, :] = jnp.broadcast_to(ends, (PACKED - 2 * BW, BW))
+
+
+def unpacked(packed):
+    row, col = unit()
+    mixed = packed[BW : 2 * BW]
+    turned = mixed.T
+    ends = packed[2 * BW : 2 * BW + 1]
+    first = jnp.where(row <= col, mixed, turned)
+    second = jnp.where(row > col, mixed, jnp.where(row < col, turned, ends))
+    return packed[:BW], first, second
+
+
+def square_kernel(value_ref, out_ref, total_ref):
+    add_square(value_ref[...], total_ref, out_ref)
+
+
+TOTAL = pltpu.VMEM((2 * BW, 2 * BW), F32)
 
 
 def tiled(width=2 * BW):
@@ -84,42 +122,78 @@
     return pltpu.with_memory_space_constraint(value, pltpu.HBM)
 
 
-def product_halves(left, right=None):
-    left = streamed(left)
-    args = (left,) if right is None else (left, right)
-    return pl.pallas_call(
-        square_kernel if right is None else product_kernel,
+def square(value):
+    return pl.pallas_call(
+        square_kernel,
+        grid=(value.shape[0] // ROW_TILE,),
+        in_specs=[tiled()],
+        out_specs=whole(PACKED),
+        out_shape=shape(PACKED),
+        scratch_shapes=[TOTAL],
+        compiler_params=PARAMS,
+    )(streamed(value))
+
+
+def product_halves(left, right):
+    return pl.pallas_call(
+        product_kernel,
         grid=(left.shape[0] // ROW_TILE,),
-        in_specs=[tiled() for _ in args],
+        in_specs=[tiled(), tiled()],
         out_specs=whole(4 * BW),
         out_shape=shape(4 * BW),
         compiler_params=PARAMS,
-    )(*args)
-
-
-def rotate_kernel(pair_ref, prev_ref, stay_ref, sent_ref, out_ref, came_ref=None, gram_ref=None):
+    )(streamed(left), right)
+
+
+def share_kernel(peers, arrived_ref, lines_ref, out_ref):
+    packed, lines = PACKED // peers, 4 * BW // peers
+    part = arrived_ref[:packed, :]
+    for i in range(1, peers):
+        part += arrived_ref[packed * i : packed * (i + 1), :]
+    for i in range(peers):
+        at = (packed + lines) * i
+        out_ref[at : at + packed, :] = part
+        out_ref[at + packed : at + packed + lines, :] = lines_ref[lines * i : lines * (i + 1), :]
+
+
+def split_kernel(peers, both_ref, packed_ref, out_ref):
+    packed, lines = PACKED // peers, 4 * BW // peers
+    part = both_ref[packed : packed + lines, :]
+    for i in range(1, peers):
+        at = (packed + lines) * i + packed
+        part += both_ref[at : at + lines, :]
+    for i in range(peers):
+        out_ref[lines * i : lines * (i + 1), :] = part
+    for i in range(peers):
+        at = (packed + lines) * i
+        packed_ref[packed * i : packed * (i + 1), :] = both_ref[at : at + packed, :]
+
+
+def rotate_kernel(pair_ref, prev_ref, stay_ref, sent_ref, out_ref, came_ref=None, gram_ref=None, total_ref=None):
     came = apply(prev_ref[...], sent_ref[: 2 * BW, :])
     stays = apply(pair_ref[...], stay_ref[: 2 * BW, :])
     out_ref[:, :BW] = stays
     out_ref[:, BW:] = came
     if gram_ref is not None:
         came_ref[...] = came
-        add_product(jnp.concatenate([stays, came], 1), None, gram_ref)
+        add_square(jnp.concatenate([stays, came], 1), total_ref, gram_ref)
 
 
 def rotate(pair, prev, stay, sent, with_gram=False):
     rows = pair.shape[0]
-    pair = streamed(pair)
     if with_gram:
         prev = streamed(prev)
-    out_specs = (tiled(), tiled(BW), whole(4 * BW))
-    out_shape = (pltpu.HBM((rows, 2 * BW), F32), shape(rows), shape(4 * BW))
+    else:
+        pair = streamed(pair)
+    out_specs = (tiled(), tiled(BW), whole(PACKED))
+    out_shape = (pltpu.HBM((rows, 2 * BW), F32), shape(rows), shape(PACKED))
     return pl.pallas_call(
         rotate_kernel,
         grid=(rows // ROW_TILE,),
         in_specs=[tiled(), tiled(), whole(stay.shape[0]), whole(sent.shape[0])],
         out_specs=out_specs if with_gram else out_specs[0],
         out_shape=out_shape if with_gram else out_shape[0],
+        scratch_shapes=[TOTAL] if with_gram else [],
         compiler_params=PARAMS,
     )(pair, prev, stay, sent)
 
@@ -173,8 +247,8 @@
 
 
 def columns_kernel(late, *refs):
-    row_of = lax.broadcasted_iota(jnp.int32, (BW, BW), 0)
-    keep = row_of == lax.broadcasted_iota(jnp.int32, (BW, BW), 1)
+    row_of, col_of = unit()
+    keep = row_of == col_of
     eye = jnp.where(keep, 1.0, 0.0).astype(F32)
 
     def upright(row):
@@ -188,10 +262,10 @@
         squares_b = sent_ref[2 * BW : 2 * BW + 1, :]
     else:
         gram_ref, rows_ref, move_out, stay_out = refs
-        gram = gram_ref[...]
-        cross = gram[2 * BW : 3 * BW]
-        squares_a = jnp.sum(jnp.where(keep, gram[:BW], 0.0), axis=0, keepdims=True)
-        squares_b = jnp.sum(jnp.where(keep, gram[3 * BW :], 0.0), axis=0, keepdims=True)
+        cross, within_a, within_b = unpacked(gram_ref[...])
+        squares_a = jnp.sum(jnp.where(keep, within_a, 0.0), axis=0, keepdims=True)
+        squares_b = gram_ref[2 * BW : 2 * BW + 1, :]
+        cross_t = cross.T
     labels_a, labels_b = rows_ref[0:1, :], rows_ref[1:2, :]
     sign, a_moves = rows_ref[2:3, :], rows_ref[3:4, :] > 0.5
     scale_a = upright(lax.rsqrt(squares_a + epsilon))
@@ -219,9 +293,9 @@
         out_ref[BW : 2 * BW, :] = bottom
         tail = jnp.where(row == 1, jnp.where(pick, labels_a, labels_b), 0.0)
         if not late:
-            image = form(gram, jnp.concatenate([top, bottom], 0))
-            squares = jnp.sum(top * image[:BW], axis=0, keepdims=True)
-            squares += jnp.sum(bottom * image[BW:], axis=0, keepdims=True)
+            image_a = mm(within_a, top) + mm(cross, bottom)
+            image_b = mm(cross_t, top) + mm(within_b, bottom)
+            squares = jnp.sum(top * image_a + bottom * image_b, axis=0, keepdims=True)
             tail = jnp.where(row == 0, jnp.maximum(squares, 0.0), tail)
         out_ref[2 * BW :, :] = tail
 
@@ -240,7 +314,7 @@
 
 
 def exchange_all(parts):
-    flat = parts.reshape(parts.shape[0], 1, -1)
+    flat = parts.reshape(lax.axis_size("rows"), 1, -1)
     return lax.all_to_all(flat, "rows", split_axis=0, concat_axis=0, tiled=True).reshape(parts.shape)
 
 
@@ -256,19 +330,25 @@
     swapped = jnp.zeros((), bool)
     pair = snapshots
     prev = to_next(pair)
-    product = product_halves(pair)
+    product = square(pair)
     for stage in range(ROUNDS // 2):
         early, late = 2 * stage, 2 * stage + 1
-        part = exchange_all(product.reshape(peers, -1, BW)).sum(axis=0)
+        arrived = exchange_all(product)
         product = product_halves(pair, prev)
-        lines = product.reshape(peers, -1, BW)
-        copies = jnp.broadcast_to(part, lines.shape)
         if late + 1 < ROUNDS:
             before = to_next(prev)
-        both = exchange_all(jnp.concatenate([copies, lines], 1))
-        gram = both[:, : lines.shape[1]].reshape(product.shape)
-        part = both[:, lines.shape[1] :].sum(axis=0)
-        cross_gram = exchange_all(jnp.broadcast_to(part, lines.shape)).reshape(product.shape)
+        both = pl.pallas_call(
+            functools.partial(share_kernel, peers),
+            out_shape=shape(PACKED + 4 * BW),
+            compiler_params=PARAMS,
+        )(arrived, product)
+        both = exchange_all(both)
+        gram, copies = pl.pallas_call(
+            functools.partial(split_kernel, peers),
+            out_shape=[shape(PACKED), shape(4 * BW)],
+            compiler_params=PARAMS,
+        )(both)
+        cross_gram = exchange_all(copies)
         first = mover[early, 0] == 0
         a_moves = first != swapped
         move, stay = columns((gram,), labels_a, labels_b, swapped, a_moves)

time: 191 us -> 202 us (1.058)
  waiting for transfers between devices: 79 us -> 87.2 us
  Pallas kernels: 42.9 us -> 46 us
  starting transfers between devices: 61.1 us -> 63.7 us
  other arithmetic: 2.48 us -> 0.32 us
    ppermute x9, waiting for transfers between devices: 3.89 us -> 30 us  [to_next(): lax.ppermute(value, 'blk', [(i, (i + 1) % peers) for i in range(peers)])]
    all_to_all x6, waiting for transfers between devices: 75.2 us -> 57.1 us  [exchange_all(): lax.all_to_all(flat, 'rows', split_axis=0, concat_axis=0, tiled=True)]
    ppermute x9, starting transfers between devices: 15.9 us -> 20.8 us  [to_next(): lax.ppermute(value, 'blk', [(i, (i + 1) % peers) for i in range(peers)])]
    pallas_call x3 -> x7, Pallas kernels: 8.25 us -> 11.5 us  [the longest x2 5.14 us: product_halves(): pl.pallas_call(product_kernel, grid=(left.shape[0] // ROW_TILE,), in_spec...]
    all_to_all x6, starting transfers between devices: 45.2 us -> 42.9 us  [exchange_all(): lax.all_to_all(flat, 'rows', split_axis=0, concat_axis=0, tiled=True)]
  transfers between devices with their start and end apart: 15 -> 15, of which waited for: 7 -> 7; matrix products, arithmetic and copies ran while one was open for 2% -> 1% of each run, Pallas kernels for 12% -> 15%
where the time goes in v2:
time: 202 us; the launch traced here: 201 us
  waiting for transfers between devices  87.2 us (43%)
  starting transfers between devices  63.7 us (32%)
  Pallas kernels  46 us (23%)
  between operations  2.2 us (1%)
    all_to_all x6, waiting for transfers between devices, exchange_all(): lax.all_to_all(flat, 'rows', split_axis=0, concat_axis=0, tiled=True)  57.1 us
    all_to_all x6, starting transfers between devices, exchange_all(): lax.all_to_all(flat, 'rows', split_axis=0, concat_axis=0, tiled=True)  42.9 us
    ppermute x9, waiting for transfers between devices, to_next(): lax.ppermute(value, 'blk', [(i, (i + 1) % peers) for i in range(peers)])  30 us
    ppermute x9, starting transfers between devices, to_next(): lax.ppermute(value, 'blk', [(i, (i + 1) % peers) for i in range(peers)])  20.8 us
    pallas_call x3, Pallas kernels, rotate(): pl.pallas_call(rotate_kernel, grid=(rows // ROW_TILE,), in_specs=[tiled()...  13.4 us
    pallas_call x4, Pallas kernels, columns(): pl.pallas_call(functools.partial(columns_kernel, len(args) > 1), out_shap...  10.8 us
    pallas_call x2, Pallas kernels, join(): pl.pallas_call(join_kernel if passed_cols is None else join_two_kernel, g...  6.88 us
    pallas_call x2, Pallas kernels, product_halves(): pl.pallas_call(product_kernel, grid=(left.shape[0] // ROW_TILE,), in_spec...  5.14 us
  transfers between devices with their start and end apart: 15, of which 7 were waited for; matrix products, arithmetic and copies ran while one was open for 1% of the time, Pallas kernels for 15%

profile of v2, /device:TPU:1, one launch (start us, length us, event | category | flops | bytes accessed | tf_op | source)
XLA Modules:
  0.0 200.8 jit_solution(11365728935864265554)
XLA Ops:
  2.6 23.3 %collective-permute-done.right_ref.prev_ref = f32[2048,256]{1,0:T(8,128)S(1)} collective-permute-done((f32[2048,256]{1,0:T(8,128)}, f32[2048,256]{1,0:T(8,128)S(1)}, u32[]{:S(2)}, u32[]{:S(2)}) %collective-permute-start) | collective-permute-done | bytes 2097184 | tf_op jit(solution)/shard_map/ppermute | solution.py:323
  28.3 3.1 %shard_map.37 = f32[320,128]{1,0:T(8,128)} custom-call(f32[2048,256]{1,0:T(8,128)} %pair_ref.1), custom_call_target="tpu_custom_call" | custom-call | tf_op jit(solution)/shard_map/pallas_call | solution.py:126
  31.3 16.3 %all-to-all-start = ((f32[64,1,640]{2,1,0:T(1,128)}), f32[64,1,640]{2,1,0:T(1,128)S(1)}, u32[]{:S(2)}, u32[]{:S(2)}) async-start(f32[64,1,640]{2,1,0:T(1,128)} %bitcast), calls=%async_computation | async-start | bytes 327680 | tf_op jit(solution)/shard_map/all_to_all | solution.py:318
  50.2 9.4 %all-to-all-done = f32[64,1,640]{2,1,0:T(1,128)S(1)} async-done(((f32[64,1,640]{2,1,0:T(1,128)}), f32[64,1,640]{2,1,0:T(1,128)S(1)}, u32[]{:S(2)}, u32[]{:S(2)}) %all-to-all-start) | async-done | bytes 163872 | tf_op jit(solution)/shard_map/all_to_all | solution.py:318
  60.5 4.6 %all-to-all-start.1 = ((f32[64,1,1664]{2,1,0:T(1,128)}), f32[64,1,1664]{2,1,0:T(1,128)S(1)}, u32[]{:S(2)}, u32[]{:S(2)}) async-start(f32[64,1,1664]{2,1,0:T(1,128)} %bitcast.2), calls=%async_computation.1 | async-start | bytes 851968 | tf_op jit(solution)/shard_map/all_to_all | solution.py:318
  67.3 12.1 %all-to-all-done.1 = f32[64,1,1664]{2,1,0:T(1,128)S(1)} async-done(((f32[64,1,1664]{2,1,0:T(1,128)}), f32[64,1,1664]{2,1,0:T(1,128)S(1)}, u32[]{:S(2)}, u32[]{:S(2)}) %all-to-all-start.1) | async-done | bytes 426016 | tf_op jit(solution)/shard_map/all_to_all | solution.py:318
  82.9 5.5 %collective-permute-start.1 = (f32[264,128]{1,0:T(8,128)S(1)}, f32[264,128]{1,0:T(8,128)S(1)}, u32[]{:S(2)}, u32[]{:S(2)}) collective-permute-start(f32[264,128]{1,0:T(8,128)S(1)} %get-tuple-element.22), channel_id=1, source_target_pairs={{0,64},{64,128},{128,192},{192,256},{256,320},{320,384},{384,448},... | collective-permute-start | bytes 405512 | tf_op jit(solution)/shard_map/ppermute | solution.py:323
  88.5 5.5 %all-to-all-start.2 = ((f32[64,1,1024]{2,1,0:T(1,128)}), f32[64,1,1024]{2,1,0:T(1,128)S(1)}, u32[]{:S(2)}, u32[]{:S(2)}) async-start(f32[64,1,1024]{2,1,0:T(1,128)} %bitcast.5), calls=%async_computation.2 | async-start | bytes 524288 | tf_op jit(solution)/shard_map/all_to_all | solution.py:318
  95.5 12.4 %all-to-all-done.2 = f32[64,1,1024]{2,1,0:T(1,128)S(1)} async-done(((f32[64,1,1024]{2,1,0:T(1,128)}), f32[64,1,1024]{2,1,0:T(1,128)S(1)}, u32[]{:S(2)}, u32[]{:S(2)}) %all-to-all-start.2) | async-done | bytes 262176 | tf_op jit(solution)/shard_map/all_to_all | solution.py:318
  107.9 2.7 %shard_map.44 = (f32[264,128]{1,0:T(8,128)S(1)}, f32[264,128]{1,0:T(8,128)S(1)}) custom-call(f32[512,128]{1,0:T(8,128)S(1)} %bitcast.33, f32[264,128]{1,0:T(8,128)S(1)} %get-tuple-element.21.stay_ref.refs_1_, f32[264,128]{1,0:T(8,128)S(1)} %collective-permute-done.1.sent_ref.refs_2_, f32[8,128]{1,0:T(8,128)S(1)} %select_select_fusion.2.refs_3_), custom_call_target="tpu_custom_call" | custom-call | tf_op jit(solution)/shard_map/pallas_call | solution.py:309
  112.2 4.2 %shard_map.42.pair_ref = f32[2048,256]{1,0:T(8,128)} custom-call(f32[2048,256]{1,0:T(8,128)} %pair_ref.1, f32[2048,256]{1,0:T(8,128)S(1)} %collective-permute-done.right_ref.prev_ref, f32[264,128]{1,0:T(8,128)S(1)} %get-tuple-element.21.stay_ref.refs_1_, f32[264,128]{1,0:T(8,128)S(1)} %collective-permute-done.1.sent_ref.refs_2_), custom_call_target="tpu_custom_call" | custom-call | tf_op jit(solution)/shard_map/pallas_call | solution.py:190
  116.4 4.4 %shard_map.43.prev_ref = f32[2048,256]{1,0:T(8,128)} custom-call(f32[2048,256]{1,0:T(8,128)S(1)} %collective-permute-done.right_ref.prev_ref, f32[264,128]{1,0:T(8,128)S(1)} %collective-permute-done.2.cols_ref, f32[2048,256]{1,0:T(8,128)} %collective-permute-done.3.other_ref, f32[264,128]{1,0:T(8,128)S(1)} %collective-permute-done.4.other_cols_ref), custom_call_target="tpu_custom_call" | custom-call | tf_op jit(solution)/shard_map/pallas_call | solution.py:216
  120.8 5.0 %shard_map.45 = (f32[2048,256]{1,0:T(8,128)}, f32[2048,128]{1,0:T(8,128)S(1)}, f32[320,128]{1,0:T(8,128)}) custom-call(f32[2048,256]{1,0:T(8,128)S(1)} %copy-done, f32[2048,256]{1,0:T(8,128)} %shard_map.43.prev_ref, f32[264,128]{1,0:T(8,128)S(1)} %get-tuple-element.24.stay_ref, f32[264,128]{1,0:T(8,128)S(1)} %collective-permute-done.5.sent_ref), custom_call_target="tpu_custom_call" | custom-call | tf_op jit(solution)/shard_map/pallas_call | solution.py:190
  126.2 4.8 %all-to-all-start.3 = ((f32[64,1,640]{2,1,0:T(1,128)}), f32[64,1,640]{2,1,0:T(1,128)S(1)}, u32[]{:S(2)}, u32[]{:S(2)}) async-start(f32[64,1,640]{2,1,0:T(1,128)} %bitcast.11), calls=%async_computation.3 | async-start | bytes 327680 | tf_op jit(solution)/shard_map/all_to_all | solution.py:318
  132.7 6.7 %collective-permute-done.6.cols_ref = f32[264,128]{1,0:T(8,128)S(1)} collective-permute-done((f32[264,128]{1,0:T(8,128)S(1)}, f32[264,128]{1,0:T(8,128)S(1)}, u32[]{:S(2)}, u32[]{:S(2)}) %collective-permute-start.6) | collective-permute-done | bytes 135200 | tf_op jit(solution)/shard_map/ppermute | solution.py:323
  145.3 7.1 %all-to-all-start.4 = ((f32[64,1,1664]{2,1,0:T(1,128)}), f32[64,1,1664]{2,1,0:T(1,128)S(1)}, u32[]{:S(2)}, u32[]{:S(2)}) async-start(f32[64,1,1664]{2,1,0:T(1,128)} %bitcast.13), calls=%async_computation.4 | async-start | bytes 851968 | tf_op jit(solution)/shard_map/all_to_all | solution.py:318
  153.3 13.1 %all-to-all-done.4 = f32[64,1,1664]{2,1,0:T(1,128)S(1)} async-done(((f32[64,1,1664]{2,1,0:T(1,128)}), f32[64,1,1664]{2,1,0:T(1,128)S(1)}, u32[]{:S(2)}, u32[]{:S(2)}) %all-to-all-start.4) | async-done | bytes 426016 | tf_op jit(solution)/shard_map/all_to_all | solution.py:318
  167.2 2.7 %shard_map.50 = (f32[264,128]{1,0:T(8,128)S(1)}, f32[264,128]{1,0:T(8,128)S(1)}) custom-call(f32[320,128]{1,0:T(8,128)S(1)} %get-tuple-element.29.refs_0_, f32[8,128]{1,0:T(8,128)S(1)} %select_select_fusion.1.refs_1_), custom_call_target="tpu_custom_call" | custom-call | tf_op jit(solution)/shard_map/pallas_call | solution.py:309
  169.9 5.8 %collective-permute-start.8 = (f32[264,128]{1,0:T(8,128)S(1)}, f32[264,128]{1,0:T(8,128)S(1)}, u32[]{:S(2)}, u32[]{:S(2)}) collective-permute-start(f32[264,128]{1,0:T(8,128)S(1)} %get-tuple-element.31), channel_id=1, source_target_pairs={{0,64},{64,128},{128,192},{192,256},{256,320},{320,384},{384,448},... | collective-permute-start | bytes 405512 | tf_op jit(solution)/shard_map/ppermute | solution.py:323
  175.7 4.6 %all-to-all-start.5 = ((f32[64,1,1024]{2,1,0:T(1,128)}), f32[64,1,1024]{2,1,0:T(1,128)S(1)}, u32[]{:S(2)}, u32[]{:S(2)}) async-start(f32[64,1,1024]{2,1,0:T(1,128)} %bitcast.19), calls=%async_computation.5 | async-start | bytes 524288 | tf_op jit(solution)/shard_map/all_to_all | solution.py:318
  180.3 4.2 %shard_map.51.pair_ref = f32[2048,256]{1,0:T(8,128)} custom-call(f32[2048,256]{1,0:T(8,128)} %get-tuple-element.26.left_ref.pair_ref, f32[2048,256]{1,0:T(8,128)S(1)} %shard_map.46.right_ref.prev_ref, f32[264,128]{1,0:T(8,128)S(1)} %get-tuple-element.30.stay_ref.refs_1_, f32[264,128]{1,0:T(8,128)S(1)} %collective-permute-done.8.sent_ref.refs_2_), custom_call_target="tpu_custom_call" | custom-call | tf_op jit(solution)/shard_map/pallas_call | solution.py:190
  184.6 10.0 %all-to-all-done.5 = f32[64,1,1024]{2,1,0:T(1,128)S(1)} async-done(((f32[64,1,1024]{2,1,0:T(1,128)}), f32[64,1,1024]{2,1,0:T(1,128)S(1)}, u32[]{:S(2)}, u32[]{:S(2)}) %all-to-all-start.5) | async-done | bytes 262176 | tf_op jit(solution)/shard_map/all_to_all | solution.py:318
  194.6 2.7 %shard_map.52 = (f32[264,128]{1,0:T(8,128)S(1)}, f32[264,128]{1,0:T(8,128)S(1)}) custom-call(f32[512,128]{1,0:T(8,128)S(1)} %bitcast.34, f32[264,128]{1,0:T(8,128)S(1)} %get-tuple-element.30.stay_ref.refs_1_, f32[264,128]{1,0:T(8,128)S(1)} %collective-permute-done.8.sent_ref.refs_2_, f32[8,128]{1,0:T(8,128)S(1)} %select_select_fusion.refs_3_), custom_call_target="tpu_custom_call" | custom-call | tf_op jit(solution)/shard_map/pallas_call | solution.py:309
  197.4 3.4 %shard_map.53 = f32[2048,256]{1,0:T(8,128)} custom-call(f32[2048,256]{1,0:T(8,128)} %shard_map.51.pair_ref, f32[264,128]{1,0:T(8,128)S(1)} %get-tuple-element.33.left_ref, f32[264,128]{1,0:T(8,128)S(1)} %get-tuple-element.34.right_ref), custom_call_target="tpu_custom_call" | custom-call | tf_op jit(solution)/shard_map/pallas_call | solution.py:235
  (49 shorter events, 24.8 us)
Async XLA Ops:
  0.0 25.9 %collective-permute-start = (f32[2048,256]{1,0:T(8,128)}, f32[2048,256]{1,0:T(8,128)S(1)}, u32[]{:S(2)}, u32[]{:S(2)}) collective-permute-start(f32[2048,256]{1,0:T(8,128)} %pair_ref.1), channel_id=1, source_target_pairs={{0,64},{64,128},{128,192},{192,256},{256,320},{320,384},{384,448},... | collective-permute-start | bytes 6291464 | tf_op jit(solution)/shard_map/ppermute | solution.py:323
  25.9 90.5 %collective-permute-start.3 = (f32[2048,256]{1,0:T(8,128)S(1)}, f32[2048,256]{1,0:T(8,128)}, u32[]{:S(2)}, u32[]{:S(2)}) collective-permute-start(f32[2048,256]{1,0:T(8,128)S(1)} %collective-permute-done.right_ref.prev_ref), channel_id=1, source_target_pairs={{0,64},{64,128},{128,192},{192,256},{256,320},{320,384},{384,448},... | collective-permute-start | bytes 6291464 | tf_op jit(solution)/shard_map/ppermute | solution.py:323
  31.3 28.3 %all-to-all-start = ((f32[64,1,640]{2,1,0:T(1,128)}), f32[64,1,640]{2,1,0:T(1,128)S(1)}, u32[]{:S(2)}, u32[]{:S(2)}) async-start(f32[64,1,640]{2,1,0:T(1,128)} %bitcast), calls=%async_computation | async-start | bytes 327680 | tf_op jit(solution)/shard_map/all_to_all | solution.py:318
  47.6 17.5 %copy-start.2 = (s32[3,1]{0,1:T(1,128)S(1)}, s32[3,1]{0,1:T(1,128)}, u32[]{:S(2)}) copy-start(s32[3,1]{0,1:T(1,128)} %param.5) | copy-start | bytes 40
  47.6 18.2 %copy-start.3 = (s32[256]{0:T(256)S(1)}, s32[256]{0:T(256)}, u32[]{:S(2)}) copy-start(s32[256]{0:T(256)} %param.4) | copy-start | bytes 3076
  60.5 19.0 %all-to-all-start.1 = ((f32[64,1,1664]{2,1,0:T(1,128)}), f32[64,1,1664]{2,1,0:T(1,128)S(1)}, u32[]{:S(2)}, u32[]{:S(2)}) async-start(f32[64,1,1664]{2,1,0:T(1,128)} %bitcast.2), calls=%async_computation.1 | async-start | bytes 851968 | tf_op jit(solution)/shard_map/all_to_all | solution.py:318
  82.9 11.3 %collective-permute-start.1 = (f32[264,128]{1,0:T(8,128)S(1)}, f32[264,128]{1,0:T(8,128)S(1)}, u32[]{:S(2)}, u32[]{:S(2)}) collective-permute-start(f32[264,128]{1,0:T(8,128)S(1)} %get-tuple-element.22), channel_id=1, source_target_pairs={{0,64},{64,128},{128,192},{192,256},{256,320},{320,384},{384,448},... | collective-permute-start | bytes 405512 | tf_op jit(solution)/shard_map/ppermute | solution.py:323
  88.5 19.4 %all-to-all-start.2 = ((f32[64,1,1024]{2,1,0:T(1,128)}), f32[64,1,1024]{2,1,0:T(1,128)S(1)}, u32[]{:S(2)}, u32[]{:S(2)}) async-start(f32[64,1,1024]{2,1,0:T(1,128)} %bitcast.5), calls=%async_computation.2 | async-start | bytes 524288 | tf_op jit(solution)/shard_map/all_to_all | solution.py:318
  93.9 22.5 %collective-permute-start.2 = (f32[264,128]{1,0:T(8,128)S(1)}, f32[264,128]{1,0:T(8,128)S(1)}, u32[]{:S(2)}, u32[]{:S(2)}) collective-permute-start(f32[264,128]{1,0:T(8,128)S(1)} %get-tuple-element.21.stay_ref.refs_1_), channel_id=1, source_target_pairs={{0,64},{64,128},{128,192},{192,256},{256,320},{320,384},{384,448},... | collective-permute-start | bytes 405512 | tf_op jit(solution)/shard_map/ppermute | solution.py:323
  94.2 22.2 %collective-permute-start.4 = (f32[264,128]{1,0:T(8,128)S(1)}, f32[264,128]{1,0:T(8,128)S(1)}, u32[]{:S(2)}, u32[]{:S(2)}) collective-permute-start(f32[264,128]{1,0:T(8,128)S(1)} %collective-permute-done.1.sent_ref.refs_2_), channel_id=1, source_target_pairs={{0,64},{64,128},{128,192},{192,256},{256,320},{320,384},{384,448},... | collective-permute-start | bytes 405512 | tf_op jit(solution)/shard_map/ppermute | solution.py:323
  110.6 10.2 %collective-permute-start.5 = (f32[264,128]{1,0:T(8,128)S(1)}, f32[264,128]{1,0:T(8,128)S(1)}, u32[]{:S(2)}, u32[]{:S(2)}) collective-permute-start(f32[264,128]{1,0:T(8,128)S(1)} %get-tuple-element.25), channel_id=1, source_target_pairs={{0,64},{64,128},{128,192},{192,256},{256,320},{320,384},{384,448},... | collective-permute-start | bytes 405512 | tf_op jit(solution)/shard_map/ppermute | solution.py:323
  116.4 4.4 %copy-start = (f32[2048,256]{1,0:T(8,128)S(1)}, f32[2048,256]{1,0:T(8,128)}, u32[]{:S(2)}) copy-start(f32[2048,256]{1,0:T(8,128)} %shard_map.42.pair_ref) | copy-start | bytes 6291460
  120.8 5.0 %copy-start.1 = (f32[264,128]{1,0:T(8,128)}, f32[264,128]{1,0:T(8,128)S(1)}, u32[]{:S(2)}) copy-start(f32[264,128]{1,0:T(8,128)S(1)} %collective-permute-done.5.sent_ref) | copy-start | bytes 405508
  125.9 13.5 %collective-permute-start.7 = (f32[2048,128]{1,0:T(8,128)S(1)}, f32[2048,128]{1,0:T(8,128)S(1)}, u32[]{:S(2)}, u32[]{:S(2)}) collective-permute-start(f32[2048,128]{1,0:T(8,128)S(1)} %get-tuple-element.27), channel_id=1, source_target_pairs={{0,64},{64,128},{128,192},{192,256},{256,320},{320,384},{384,448},... | collective-permute-start | bytes 3145736 | tf_op jit(solution)/shard_map/ppermute | solution.py:323
  126.2 18.3 %all-to-all-start.3 = ((f32[64,1,640]{2,1,0:T(1,128)}), f32[64,1,640]{2,1,0:T(1,128)S(1)}, u32[]{:S(2)}, u32[]{:S(2)}) async-start(f32[64,1,640]{2,1,0:T(1,128)} %bitcast.11), calls=%async_computation.3 | async-start | bytes 327680 | tf_op jit(solution)/shard_map/all_to_all | solution.py:318
  131.0 8.4 %collective-permute-start.6 = (f32[264,128]{1,0:T(8,128)S(1)}, f32[264,128]{1,0:T(8,128)S(1)}, u32[]{:S(2)}, u32[]{:S(2)}) collective-permute-start(f32[264,128]{1,0:T(8,128)S(1)} %get-tuple-element.24.stay_ref), channel_id=1, source_target_pairs={{0,64},{64,128},{128,192},{192,256},{256,320},{320,384},{384,448},... | collective-permute-start | bytes 405512 | tf_op jit(solution)/shard_map/ppermute | solution.py:323
  145.3 21.1 %all-to-all-start.4 = ((f32[64,1,1664]{2,1,0:T(1,128)}), f32[64,1,1664]{2,1,0:T(1,128)S(1)}, u32[]{:S(2)}, u32[]{:S(2)}) async-start(f32[64,1,1664]{2,1,0:T(1,128)} %bitcast.13), calls=%async_computation.4 | async-start | bytes 851968 | tf_op jit(solution)/shard_map/all_to_all | solution.py:318
  169.9 10.4 %collective-permute-start.8 = (f32[264,128]{1,0:T(8,128)S(1)}, f32[264,128]{1,0:T(8,128)S(1)}, u32[]{:S(2)}, u32[]{:S(2)}) collective-permute-start(f32[264,128]{1,0:T(8,128)S(1)} %get-tuple-element.31), channel_id=1, source_target_pairs={{0,64},{64,128},{128,192},{192,256},{256,320},{320,384},{384,448},... | collective-permute-start | bytes 405512 | tf_op jit(solution)/shard_map/ppermute | solution.py:323
  175.7 19.0 %all-to-all-start.5 = ((f32[64,1,1024]{2,1,0:T(1,128)}), f32[64,1,1024]{2,1,0:T(1,128)S(1)}, u32[]{:S(2)}, u32[]{:S(2)}) async-start(f32[64,1,1024]{2,1,0:T(1,128)} %bitcast.19), calls=%async_computation.5 | async-start | bytes 524288 | tf_op jit(solution)/shard_map/all_to_all | solution.py:318

commit v3 on v2

--- a/solution.py
+++ b/solution.py
@@ -12,6 +12,7 @@
 NS_STEPS = 3
 ROW_TILE = 1024
 PACKED = 5 * 64
+PADDED = 8 * 64
 PARAMS = pltpu.CompilerParams(vmem_limit_bytes=16 * 2**20)
 
 epsilon = 1e-06
@@ -83,10 +84,18 @@
     def _():
         row, col = unit()
         second = total_ref[BW:, BW:]
-        out_ref[:BW, :] = total_ref[:BW, BW:]
-        out_ref[BW : 2 * BW, :] = jnp.where(row <= col, total_ref[:BW, :BW], second)
+        corner = total_ref[:BW, BW:]
+        mixed = jnp.where(row <= col, total_ref[:BW, :BW], second)
         ends = jnp.sum(jnp.where(row == col, second, 0.0), axis=0, keepdims=True)
-        out_ref[2 * BW :, :] = jnp.broadcast_to(ends, (PACKED - 2 * BW, BW))
+        ends = jnp.broadcast_to(ends, (PACKED - 2 * BW, BW))
+        total_ref[:BW, :BW] = corner
+        total_ref[BW:, :BW] = mixed
+        for i in range(PADDED // 8):
+            low = 5 * i
+            inner = min(max(2 * BW - low, 0), 5)
+            if inner:
+                out_ref[8 * i : 8 * i + inner, :] = total_ref[low : low + inner, :BW]
+            out_ref[8 * i + inner : 8 * (i + 1), :] = ends[: 8 - inner, :]
 
 
 def unpacked(packed):
@@ -127,8 +136,8 @@
         square_kernel,
         grid=(value.shape[0] // ROW_TILE,),
         in_specs=[tiled()],
-        out_specs=whole(PACKED),
-        out_shape=shape(PACKED),
+        out_specs=whole(PADDED),
+        out_shape=shape(PADDED),
         scratch_shapes=[TOTAL],
         compiler_params=PARAMS,
     )(streamed(value))
@@ -147,9 +156,11 @@
 
 def share_kernel(peers, arrived_ref, lines_ref, out_ref):
     packed, lines = PACKED // peers, 4 * BW // peers
-    part = arrived_ref[:packed, :]
+    padded = PADDED // peers
+    part = arrived_ref[:padded, :]
     for i in range(1, peers):
-        part += arrived_ref[packed * i : packed * (i + 1), :]
+        part += arrived_ref[padded * i : padded * (i + 1), :]
+    part = jnp.concatenate([part[8 * k : 8 * k + 5] for k in range(padded // 8)], 0)
     for i in range(peers):
         at = (packed + lines) * i
         out_ref[at : at + packed, :] = part
@@ -185,8 +196,8 @@
         prev = streamed(prev)
     else:
         pair = streamed(pair)
-    out_specs = (tiled(), tiled(BW), whole(PACKED))
-    out_shape = (pltpu.HBM((rows, 2 * BW), F32), shape(rows), shape(PACKED))
+    out_specs = (tiled(), tiled(BW), whole(PADDED))
+    out_shape = (pltpu.HBM((rows, 2 * BW), F32), shape(rows), shape(PADDED))
     return pl.pallas_call(
         rotate_kernel,
         grid=(rows // ROW_TILE,),
@@ -211,7 +222,7 @@
 def join(prev, cols, passed, passed_cols=None):
     rows = prev.shape[0]
     if passed_cols is None:
-        prev = streamed(prev)
+        prev, passed = streamed(prev), streamed(passed)
     args = (prev, cols, passed) if passed_cols is None else (prev, cols, passed, passed_cols)
     return pl.pallas_call(
         join_kernel if passed_cols is None else join_two_kernel,
@@ -230,7 +241,6 @@
 
 
 def last(pair, left, right):
-    pair = streamed(pair)
     rows = pair.shape[0]
     return pl.pallas_call(
         last_kernel,

time: 202 us -> 184 us (0.911)
  waiting for transfers between devices: 87.2 us -> 66.7 us
  starting transfers between devices: 63.7 us -> 66.7 us
    ppermute x9, waiting for transfers between devices: 30 us -> 10.4 us  [to_next(): lax.ppermute(value, 'blk', [(i, (i + 1) % peers) for i in range(peers)])]
    all_to_all x6, starting transfers between devices: 42.9 us -> 48.9 us  [exchange_all(): lax.all_to_all(flat, 'rows', split_axis=0, concat_axis=0, tiled=True)]
    ppermute x9, starting transfers between devices: 20.8 us -> 17.7 us  [to_next(): lax.ppermute(value, 'blk', [(i, (i + 1) % peers) for i in range(peers)])]
  transfers between devices with their start and end apart: 15 -> 15, of which waited for: 7 -> 8; matrix products, arithmetic and copies ran while one was open for 1% -> 1% of each run, Pallas kernels for 15% -> 17%
where the time goes in v3:
time: 184 us; the launch traced here: 183 us
  starting transfers between devices  66.7 us (36%)
  waiting for transfers between devices  66.7 us (36%)
  Pallas kernels  45 us (24%)
  local copies, waits for them, and re-layouts  2.29 us (1%)
  between operations  2.2 us (1%)
    all_to_all x6, waiting for transfers between devices, exchange_all(): lax.all_to_all(flat, 'rows', split_axis=0, concat_axis=0, tiled=True)  56.3 us
    all_to_all x6, starting transfers between devices, exchange_all(): lax.all_to_all(flat, 'rows', split_axis=0, concat_axis=0, tiled=True)  48.9 us
    ppermute x9, starting transfers between devices, to_next(): lax.ppermute(value, 'blk', [(i, (i + 1) % peers) for i in range(peers)])  17.7 us
    pallas_call x3, Pallas kernels, rotate(): pl.pallas_call(rotate_kernel, grid=(rows // ROW_TILE,), in_specs=[tiled()...  13.4 us
    pallas_call x4, Pallas kernels, columns(): pl.pallas_call(functools.partial(columns_kernel, len(args) > 1), out_shap...  10.8 us
    ppermute x9, waiting for transfers between devices, to_next(): lax.ppermute(value, 'blk', [(i, (i + 1) % peers) for i in range(peers)])  10.4 us
    pallas_call x2, Pallas kernels, join(): pl.pallas_call(join_kernel if passed_cols is None else join_two_kernel, g...  7.01 us
    pallas_call x2, Pallas kernels, product_halves(): pl.pallas_call(product_kernel, grid=(left.shape[0] // ROW_TILE,), in_spec...  5.13 us
  transfers between devices with their start and end apart: 15, of which 8 were waited for; matrix products, arithmetic and copies ran while one was open for 1% of the time, Pallas kernels for 17%

profile of v3, /device:TPU:1, one launch (start us, length us, event | category | flops | bytes accessed | tf_op | source)
XLA Modules:
  0.0 183.2 jit_solution(16598123369300562344)
XLA Ops:
  2.6 3.2 %shard_map.37 = f32[512,128]{1,0:T(8,128)} custom-call(f32[2048,256]{1,0:T(8,128)} %pair_ref.1), custom_call_target="tpu_custom_call" | custom-call | tf_op jit(solution)/shard_map/pallas_call | solution.py:135
  5.7 16.3 %all-to-all-start = ((f32[64,1,1024]{2,1,0:T(1,128)}), f32[64,1,1024]{2,1,0:T(1,128)S(1)}, u32[]{:S(2)}, u32[]{:S(2)}) async-start(f32[64,1,1024]{2,1,0:T(1,128)} %bitcast), calls=%async_computation | async-start | bytes 524288 | tf_op jit(solution)/shard_map/all_to_all | solution.py:328
  22.1 3.8 %collective-permute-done.right_ref.prev_ref = f32[2048,256]{1,0:T(8,128)S(1)} collective-permute-done((f32[2048,256]{1,0:T(8,128)}, f32[2048,256]{1,0:T(8,128)S(1)}, u32[]{:S(2)}, u32[]{:S(2)}) %collective-permute-start) | collective-permute-done | bytes 2097184 | tf_op jit(solution)/shard_map/ppermute | solution.py:333
  30.8 5.6 %all-to-all-done = f32[64,1,1024]{2,1,0:T(1,128)S(1)} async-done(((f32[64,1,1024]{2,1,0:T(1,128)}), f32[64,1,1024]{2,1,0:T(1,128)S(1)}, u32[]{:S(2)}, u32[]{:S(2)}) %all-to-all-start) | async-done | bytes 262176 | tf_op jit(solution)/shard_map/all_to_all | solution.py:328
  37.2 10.8 %all-to-all-start.1 = ((f32[64,1,1664]{2,1,0:T(1,128)}), f32[64,1,1664]{2,1,0:T(1,128)S(1)}, u32[]{:S(2)}, u32[]{:S(2)}) async-start(f32[64,1,1664]{2,1,0:T(1,128)} %bitcast.2), calls=%async_computation.1 | async-start | bytes 851968 | tf_op jit(solution)/shard_map/all_to_all | solution.py:328
  50.2 14.0 %all-to-all-done.1 = f32[64,1,1664]{2,1,0:T(1,128)S(1)} async-done(((f32[64,1,1664]{2,1,0:T(1,128)}), f32[64,1,1664]{2,1,0:T(1,128)S(1)}, u32[]{:S(2)}, u32[]{:S(2)}) %all-to-all-start.1) | async-done | bytes 426016 | tf_op jit(solution)/shard_map/all_to_all | solution.py:328
  65.0 2.7 %shard_map.41 = (f32[264,128]{1,0:T(8,128)S(1)}, f32[264,128]{1,0:T(8,128)S(1)}) custom-call(f32[320,128]{1,0:T(8,128)S(1)} %get-tuple-element.20.refs_0_, f32[8,128]{1,0:T(8,128)S(1)} %select_select_fusion.3.refs_1_), custom_call_target="tpu_custom_call" | custom-call | tf_op jit(solution)/shard_map/pallas_call | solution.py:319
  69.3 5.8 %all-to-all-start.2 = ((f32[64,1,1024]{2,1,0:T(1,128)}), f32[64,1,1024]{2,1,0:T(1,128)S(1)}, u32[]{:S(2)}, u32[]{:S(2)}) async-start(f32[64,1,1024]{2,1,0:T(1,128)} %bitcast.5), calls=%async_computation.2 | async-start | bytes 524288 | tf_op jit(solution)/shard_map/all_to_all | solution.py:328
  77.3 11.9 %all-to-all-done.2 = f32[64,1,1024]{2,1,0:T(1,128)S(1)} async-done(((f32[64,1,1024]{2,1,0:T(1,128)}), f32[64,1,1024]{2,1,0:T(1,128)S(1)}, u32[]{:S(2)}, u32[]{:S(2)}) %all-to-all-start.2) | async-done | bytes 262176 | tf_op jit(solution)/shard_map/all_to_all | solution.py:328
  89.2 2.7 %shard_map.44 = (f32[264,128]{1,0:T(8,128)S(1)}, f32[264,128]{1,0:T(8,128)S(1)}) custom-call(f32[512,128]{1,0:T(8,128)S(1)} %bitcast.33, f32[264,128]{1,0:T(8,128)S(1)} %get-tuple-element.21.stay_ref.refs_1_, f32[264,128]{1,0:T(8,128)S(1)} %collective-permute-done.1.sent_ref.refs_2_, f32[8,128]{1,0:T(8,128)S(1)} %select_select_fusion.2.refs_3_), custom_call_target="tpu_custom_call" | custom-call | tf_op jit(solution)/shard_map/pallas_call | solution.py:319
  93.0 4.2 %shard_map.42.pair_ref = f32[2048,256]{1,0:T(8,128)} custom-call(f32[2048,256]{1,0:T(8,128)} %pair_ref.1, f32[2048,256]{1,0:T(8,128)S(1)} %collective-permute-done.right_ref.prev_ref, f32[264,128]{1,0:T(8,128)S(1)} %get-tuple-element.21.stay_ref.refs_1_, f32[264,128]{1,0:T(8,128)S(1)} %collective-permute-done.1.sent_ref.refs_2_), custom_call_target="tpu_custom_call" | custom-call | tf_op jit(solution)/shard_map/pallas_call | solution.py:201
  97.3 4.4 %shard_map.43.prev_ref = f32[2048,256]{1,0:T(8,128)} custom-call(f32[2048,256]{1,0:T(8,128)S(1)} %collective-permute-done.right_ref.prev_ref, f32[264,128]{1,0:T(8,128)S(1)} %collective-permute-done.2.cols_ref, f32[2048,256]{1,0:T(8,128)} %collective-permute-done.3.other_ref, f32[264,128]{1,0:T(8,128)S(1)} %collective-permute-done.4.other_cols_ref), custom_call_target="tpu_custom_call" | custom-call | tf_op jit(solution)/shard_map/pallas_call | solution.py:227
  101.6 5.1 %shard_map.45 = (f32[2048,256]{1,0:T(8,128)}, f32[2048,128]{1,0:T(8,128)S(1)}, f32[512,128]{1,0:T(8,128)}) custom-call(f32[2048,256]{1,0:T(8,128)S(1)} %copy-done, f32[2048,256]{1,0:T(8,128)} %shard_map.43.prev_ref, f32[264,128]{1,0:T(8,128)S(1)} %get-tuple-element.24.stay_ref, f32[264,128]{1,0:T(8,128)S(1)} %collective-permute-done.5.sent_ref), custom_call_target="tpu_custom_call" | custom-call | tf_op jit(solution)/shard_map/pallas_call | solution.py:201
  108.1 4.8 %all-to-all-start.3 = ((f32[64,1,1024]{2,1,0:T(1,128)}), f32[64,1,1024]{2,1,0:T(1,128)S(1)}, u32[]{:S(2)}, u32[]{:S(2)}) async-start(f32[64,1,1024]{2,1,0:T(1,128)} %bitcast.11), calls=%async_computation.3 | async-start | bytes 524288 | tf_op jit(solution)/shard_map/all_to_all | solution.py:328
  114.7 6.6 %collective-permute-done.6.cols_ref = f32[264,128]{1,0:T(8,128)S(1)} collective-permute-done((f32[264,128]{1,0:T(8,128)S(1)}, f32[264,128]{1,0:T(8,128)S(1)}, u32[]{:S(2)}, u32[]{:S(2)}) %collective-permute-start.6) | collective-permute-done | bytes 135200 | tf_op jit(solution)/shard_map/ppermute | solution.py:333
  121.3 2.6 %shard_map.46.right_ref.prev_ref = f32[2048,256]{1,0:T(8,128)S(1)} custom-call(f32[2048,256]{1,0:T(8,128)} %shard_map.43.prev_ref, f32[264,128]{1,0:T(8,128)S(1)} %collective-permute-done.6.cols_ref, f32[2048,128]{1,0:T(8,128)} %collective-permute-done.7.passed_ref), custom_call_target="tpu_custom_call" | custom-call | tf_op jit(solution)/shard_map/pallas_call | solution.py:227
  127.9 6.7 %all-to-all-start.4 = ((f32[64,1,1664]{2,1,0:T(1,128)}), f32[64,1,1664]{2,1,0:T(1,128)S(1)}, u32[]{:S(2)}, u32[]{:S(2)}) async-start(f32[64,1,1664]{2,1,0:T(1,128)} %bitcast.13), calls=%async_computation.4 | async-start | bytes 851968 | tf_op jit(solution)/shard_map/all_to_all | solution.py:328
  134.7 14.1 %all-to-all-done.4 = f32[64,1,1664]{2,1,0:T(1,128)S(1)} async-done(((f32[64,1,1664]{2,1,0:T(1,128)}), f32[64,1,1664]{2,1,0:T(1,128)S(1)}, u32[]{:S(2)}, u32[]{:S(2)}) %all-to-all-start.4) | async-done | bytes 426016 | tf_op jit(solution)/shard_map/all_to_all | solution.py:328
  149.7 2.7 %shard_map.50 = (f32[264,128]{1,0:T(8,128)S(1)}, f32[264,128]{1,0:T(8,128)S(1)}) custom-call(f32[320,128]{1,0:T(8,128)S(1)} %get-tuple-element.29.refs_0_, f32[8,128]{1,0:T(8,128)S(1)} %select_select_fusion.1.refs_1_), custom_call_target="tpu_custom_call" | custom-call | tf_op jit(solution)/shard_map/pallas_call | solution.py:319
  152.3 5.3 %collective-permute-start.8 = (f32[264,128]{1,0:T(8,128)S(1)}, f32[264,128]{1,0:T(8,128)S(1)}, u32[]{:S(2)}, u32[]{:S(2)}) collective-permute-start(f32[264,128]{1,0:T(8,128)S(1)} %get-tuple-element.31), channel_id=1, source_target_pairs={{0,64},{64,128},{128,192},{192,256},{256,320},{320,384},{384,448},... | collective-permute-start | bytes 405512 | tf_op jit(solution)/shard_map/ppermute | solution.py:333
  157.7 4.6 %all-to-all-start.5 = ((f32[64,1,1024]{2,1,0:T(1,128)}), f32[64,1,1024]{2,1,0:T(1,128)S(1)}, u32[]{:S(2)}, u32[]{:S(2)}) async-start(f32[64,1,1024]{2,1,0:T(1,128)} %bitcast.19), calls=%async_computation.5 | async-start | bytes 524288 | tf_op jit(solution)/shard_map/all_to_all | solution.py:328
  162.3 4.2 %shard_map.51.pair_ref = f32[2048,256]{1,0:T(8,128)} custom-call(f32[2048,256]{1,0:T(8,128)} %get-tuple-element.26.left_ref.pair_ref, f32[2048,256]{1,0:T(8,128)S(1)} %shard_map.46.right_ref.prev_ref, f32[264,128]{1,0:T(8,128)S(1)} %get-tuple-element.30.stay_ref.refs_1_, f32[264,128]{1,0:T(8,128)S(1)} %collective-permute-done.8.sent_ref.refs_2_), custom_call_target="tpu_custom_call" | custom-call | tf_op jit(solution)/shard_map/pallas_call | solution.py:201
  166.6 10.2 %all-to-all-done.5 = f32[64,1,1024]{2,1,0:T(1,128)S(1)} async-done(((f32[64,1,1024]{2,1,0:T(1,128)}), f32[64,1,1024]{2,1,0:T(1,128)S(1)}, u32[]{:S(2)}, u32[]{:S(2)}) %all-to-all-start.5) | async-done | bytes 262176 | tf_op jit(solution)/shard_map/all_to_all | solution.py:328
  176.7 2.7 %shard_map.52 = (f32[264,128]{1,0:T(8,128)S(1)}, f32[264,128]{1,0:T(8,128)S(1)}) custom-call(f32[512,128]{1,0:T(8,128)S(1)} %bitcast.34, f32[264,128]{1,0:T(8,128)S(1)} %get-tuple-element.30.stay_ref.refs_1_, f32[264,128]{1,0:T(8,128)S(1)} %collective-permute-done.8.sent_ref.refs_2_, f32[8,128]{1,0:T(8,128)S(1)} %select_select_fusion.refs_3_), custom_call_target="tpu_custom_call" | custom-call | tf_op jit(solution)/shard_map/pallas_call | solution.py:319
  (49 shorter events, 26.2 us)
Async XLA Ops:
  0.0 25.9 %collective-permute-start = (f32[2048,256]{1,0:T(8,128)}, f32[2048,256]{1,0:T(8,128)S(1)}, u32[]{:S(2)}, u32[]{:S(2)}) collective-permute-start(f32[2048,256]{1,0:T(8,128)} %pair_ref.1), channel_id=1, source_target_pairs={{0,64},{64,128},{128,192},{192,256},{256,320},{320,384},{384,448},... | collective-permute-start | bytes 6291464 | tf_op jit(solution)/shard_map/ppermute | solution.py:333
  5.7 30.6 %all-to-all-start = ((f32[64,1,1024]{2,1,0:T(1,128)}), f32[64,1,1024]{2,1,0:T(1,128)S(1)}, u32[]{:S(2)}, u32[]{:S(2)}) async-start(f32[64,1,1024]{2,1,0:T(1,128)} %bitcast), calls=%async_computation | async-start | bytes 524288 | tf_op jit(solution)/shard_map/all_to_all | solution.py:328
  22.1 25.9 %copy-start.2 = (s32[3,1]{0,1:T(1,128)S(1)}, s32[3,1]{0,1:T(1,128)}, u32[]{:S(2)}) copy-start(s32[3,1]{0,1:T(1,128)} %param.5) | copy-start | bytes 40
  22.1 26.6 %copy-start.3 = (s32[256]{0:T(256)S(1)}, s32[256]{0:T(256)}, u32[]{:S(2)}) copy-start(s32[256]{0:T(256)} %param.4) | copy-start | bytes 3076
  25.9 71.4 %collective-permute-start.3 = (f32[2048,256]{1,0:T(8,128)S(1)}, f32[2048,256]{1,0:T(8,128)}, u32[]{:S(2)}, u32[]{:S(2)}) collective-permute-start(f32[2048,256]{1,0:T(8,128)S(1)} %collective-permute-done.right_ref.prev_ref), channel_id=1, source_target_pairs={{0,64},{64,128},{128,192},{192,256},{256,320},{320,384},{384,448},... | collective-permute-start | bytes 6291464 | tf_op jit(solution)/shard_map/ppermute | solution.py:333
  37.2 27.0 %all-to-all-start.1 = ((f32[64,1,1664]{2,1,0:T(1,128)}), f32[64,1,1664]{2,1,0:T(1,128)S(1)}, u32[]{:S(2)}, u32[]{:S(2)}) async-start(f32[64,1,1664]{2,1,0:T(1,128)} %bitcast.2), calls=%async_computation.1 | async-start | bytes 851968 | tf_op jit(solution)/shard_map/all_to_all | solution.py:328
  67.7 8.0 %collective-permute-start.1 = (f32[264,128]{1,0:T(8,128)S(1)}, f32[264,128]{1,0:T(8,128)S(1)}, u32[]{:S(2)}, u32[]{:S(2)}) collective-permute-start(f32[264,128]{1,0:T(8,128)S(1)} %get-tuple-element.22), channel_id=1, source_target_pairs={{0,64},{64,128},{128,192},{192,256},{256,320},{320,384},{384,448},... | collective-permute-start | bytes 405512 | tf_op jit(solution)/shard_map/ppermute | solution.py:333
  69.3 19.8 %all-to-all-start.2 = ((f32[64,1,1024]{2,1,0:T(1,128)}), f32[64,1,1024]{2,1,0:T(1,128)S(1)}, u32[]{:S(2)}, u32[]{:S(2)}) async-start(f32[64,1,1024]{2,1,0:T(1,128)} %bitcast.5), calls=%async_computation.2 | async-start | bytes 524288 | tf_op jit(solution)/shard_map/all_to_all | solution.py:328
  75.2 22.1 %collective-permute-start.2 = (f32[264,128]{1,0:T(8,128)S(1)}, f32[264,128]{1,0:T(8,128)S(1)}, u32[]{:S(2)}, u32[]{:S(2)}) collective-permute-start(f32[264,128]{1,0:T(8,128)S(1)} %get-tuple-element.21.stay_ref.refs_1_), channel_id=1, source_target_pairs={{0,64},{64,128},{128,192},{192,256},{256,320},{320,384},{384,448},... | collective-permute-start | bytes 405512 | tf_op jit(solution)/shard_map/ppermute | solution.py:333
  75.6 21.6 %collective-permute-start.4 = (f32[264,128]{1,0:T(8,128)S(1)}, f32[264,128]{1,0:T(8,128)S(1)}, u32[]{:S(2)}, u32[]{:S(2)}) collective-permute-start(f32[264,128]{1,0:T(8,128)S(1)} %collective-permute-done.1.sent_ref.refs_2_), channel_id=1, source_target_pairs={{0,64},{64,128},{128,192},{192,256},{256,320},{320,384},{384,448},... | collective-permute-start | bytes 405512 | tf_op jit(solution)/shard_map/ppermute | solution.py:333
  91.9 9.7 %collective-permute-start.5 = (f32[264,128]{1,0:T(8,128)S(1)}, f32[264,128]{1,0:T(8,128)S(1)}, u32[]{:S(2)}, u32[]{:S(2)}) collective-permute-start(f32[264,128]{1,0:T(8,128)S(1)} %get-tuple-element.25), channel_id=1, source_target_pairs={{0,64},{64,128},{128,192},{192,256},{256,320},{320,384},{384,448},... | collective-permute-start | bytes 405512 | tf_op jit(solution)/shard_map/ppermute | solution.py:333
  97.2 4.4 %copy-start = (f32[2048,256]{1,0:T(8,128)S(1)}, f32[2048,256]{1,0:T(8,128)}, u32[]{:S(2)}) copy-start(f32[2048,256]{1,0:T(8,128)} %shard_map.42.pair_ref) | copy-start | bytes 6291460
  106.7 14.6 %collective-permute-start.7 = (f32[2048,128]{1,0:T(8,128)S(1)}, f32[2048,128]{1,0:T(8,128)}, u32[]{:S(2)}, u32[]{:S(2)}) collective-permute-start(f32[2048,128]{1,0:T(8,128)S(1)} %get-tuple-element.27), channel_id=1, source_target_pairs={{0,64},{64,128},{128,192},{192,256},{256,320},{320,384},{384,448},... | collective-permute-start | bytes 3145736 | tf_op jit(solution)/shard_map/ppermute | solution.py:333
  108.1 19.0 %all-to-all-start.3 = ((f32[64,1,1024]{2,1,0:T(1,128)}), f32[64,1,1024]{2,1,0:T(1,128)S(1)}, u32[]{:S(2)}, u32[]{:S(2)}) async-start(f32[64,1,1024]{2,1,0:T(1,128)} %bitcast.11), calls=%async_computation.3 | async-start | bytes 524288 | tf_op jit(solution)/shard_map/all_to_all | solution.py:328
  112.9 8.4 %collective-permute-start.6 = (f32[264,128]{1,0:T(8,128)S(1)}, f32[264,128]{1,0:T(8,128)S(1)}, u32[]{:S(2)}, u32[]{:S(2)}) collective-permute-start(f32[264,128]{1,0:T(8,128)S(1)} %get-tuple-element.24.stay_ref), channel_id=1, source_target_pairs={{0,64},{64,128},{128,192},{192,256},{256,320},{320,384},{384,448},... | collective-permute-start | bytes 405512 | tf_op jit(solution)/shard_map/ppermute | solution.py:333
  127.9 20.9 %all-to-all-start.4 = ((f32[64,1,1664]{2,1,0:T(1,128)}), f32[64,1,1664]{2,1,0:T(1,128)S(1)}, u32[]{:S(2)}, u32[]{:S(2)}) async-start(f32[64,1,1664]{2,1,0:T(1,128)} %bitcast.13), calls=%async_computation.4 | async-start | bytes 851968 | tf_op jit(solution)/shard_map/all_to_all | solution.py:328
  152.3 9.9 %collective-permute-start.8 = (f32[264,128]{1,0:T(8,128)S(1)}, f32[264,128]{1,0:T(8,128)S(1)}, u32[]{:S(2)}, u32[]{:S(2)}) collective-permute-start(f32[264,128]{1,0:T(8,128)S(1)} %get-tuple-element.31), channel_id=1, source_target_pairs={{0,64},{64,128},{128,192},{192,256},{256,320},{320,384},{384,448},... | collective-permute-start | bytes 405512 | tf_op jit(solution)/shard_map/ppermute | solution.py:333
  157.7 19.1 %all-to-all-start.5 = ((f32[64,1,1024]{2,1,0:T(1,128)}), f32[64,1,1024]{2,1,0:T(1,128)S(1)}, u32[]{:S(2)}, u32[]{:S(2)}) async-start(f32[64,1,1024]{2,1,0:T(1,128)} %bitcast.19), calls=%async_computation.5 | async-start | bytes 524288 | tf_op jit(solution)/shard_map/all_to_all | solution.py:328
  179.5 1.6 copy-start.1

commit v4 on v3

--- a/solution.py
+++ b/solution.py
@@ -52,18 +52,31 @@
     return row, lax.broadcasted_iota(jnp.int32, (BW, BW), 1)
 
 
-def product_kernel(left_ref, right_ref, out_ref):
-    left_high, left_low = in_two(left_ref[...])
-    right_high, right_low = in_two(right_ref[...])
+def add_product(left, right, *out_refs):
+    left_high, left_low = in_two(left)
+    right_high, right_low = in_two(right)
     cross = transposed_dot(left_high, right_low) + transposed_dot(left_low, right_high)
     value = transposed_dot(left_high, right_high) + cross
-
-    @pl.when(pl.program_id(0) == 0)
-    def _():
-        out_ref[...] = jnp.zeros_like(out_ref)
-
-    out_ref[: 2 * BW, :] += value[:, :BW]
-    out_ref[2 * BW :, :] += value[:, BW:]
+    for k, out_ref in enumerate(out_refs):
+        block = value[:, BW * k : BW * (k + 1)]
+
+        @pl.when(pl.program_id(0) == 0)
+        def _(out_ref=out_ref, block=block):
+            out_ref[...] = block
+
+        @pl.when(pl.program_id(0) > 0)
+        def _(out_ref=out_ref, block=block):
+            out_ref[...] += block
+
+
+def product_kernel(left_ref, right_ref, *out_refs):
+    add_product(left_ref[...], right_ref[...], *out_refs)
+
+
+def stay_product_kernel(left_ref, prev_ref, cols_ref, out_ref, product_ref):
+    value = apply(prev_ref[...], cols_ref[: 2 * BW, :])
+    out_ref[...] = value
+    add_product(left_ref[...], value, product_ref)
 
 
 def add_square(value, total_ref, out_ref):
@@ -143,18 +156,31 @@
     )(streamed(value))
 
 
-def product_halves(left, right):
+def product(left, right):
+    blocks = right.shape[1] // BW
     return pl.pallas_call(
         product_kernel,
         grid=(left.shape[0] // ROW_TILE,),
-        in_specs=[tiled(), tiled()],
-        out_specs=whole(4 * BW),
-        out_shape=shape(4 * BW),
+        in_specs=[tiled(), tiled(right.shape[1])],
+        out_specs=[whole(2 * BW)] * blocks,
+        out_shape=[shape(2 * BW)] * blocks,
         compiler_params=PARAMS,
     )(streamed(left), right)
 
 
-def share_kernel(peers, arrived_ref, lines_ref, out_ref):
+def stay_product(left, prev, cols):
+    rows = left.shape[0]
+    return pl.pallas_call(
+        stay_product_kernel,
+        grid=(rows // ROW_TILE,),
+        in_specs=[tiled(), tiled(), whole(cols.shape[0])],
+        out_specs=[tiled(BW), whole(2 * BW)],
+        out_shape=[shape(rows), shape(2 * BW)],
+        compiler_params=PARAMS,
+    )(streamed(left), streamed(prev), cols)
+
+
+def share_kernel(peers, arrived_ref, first_ref, second_ref, out_ref):
     packed, lines = PACKED // peers, 4 * BW // peers
     padded = PADDED // peers
     part = arrived_ref[:padded, :]
@@ -164,7 +190,9 @@
     for i in range(peers):
         at = (packed + lines) * i
         out_ref[at : at + packed, :] = part
-        out_ref[at + packed : at + packed + lines, :] = lines_ref[lines * i : lines * (i + 1), :]
+        half = peers // 2
+        lines_ref, line = (first_ref, lines * i) if i < half else (second_ref, lines * (i - half))
+        out_ref[at + packed : at + packed + lines, :] = lines_ref[line : line + lines, :]
 
 
 def split_kernel(peers, both_ref, packed_ref, out_ref):
@@ -180,56 +208,66 @@
         packed_ref[packed * i : packed * (i + 1), :] = both_ref[at : at + packed, :]
 
 
-def rotate_kernel(pair_ref, prev_ref, stay_ref, sent_ref, out_ref, came_ref=None, gram_ref=None, total_ref=None):
-    came = apply(prev_ref[...], sent_ref[: 2 * BW, :])
+def rotated(pair_ref, prev_refs, stay_ref, sent_ref, out_ref):
+    width = 2 * BW // len(prev_refs)
+    came = 0.0
+    for k, prev_ref in enumerate(prev_refs):
+        came += apply(prev_ref[...], sent_ref[width * k : width * (k + 1), :])
     stays = apply(pair_ref[...], stay_ref[: 2 * BW, :])
     out_ref[:, :BW] = stays
     out_ref[:, BW:] = came
-    if gram_ref is not None:
-        came_ref[...] = came
-        add_square(jnp.concatenate([stays, came], 1), total_ref, gram_ref)
-
-
-def rotate(pair, prev, stay, sent, with_gram=False):
+    return stays, came
+
+
+def rotate_kernel(pair_ref, *refs):
+    *prev_refs, stay_ref, sent_ref, out_ref = refs
+    rotated(pair_ref, prev_refs, stay_ref, sent_ref, out_ref)
+
+
+def rotate_square_kernel(pair_ref, prev_ref, stay_ref, sent_ref, out_ref, came_ref, square_ref, total_ref):
+    stays, came = rotated(pair_ref, [prev_ref], stay_ref, sent_ref, out_ref)
+    came_ref[...] = came
+    add_square(jnp.concatenate([stays, came], 1), total_ref, square_ref)
+
+
+def rotate(pair, prev, stay, sent):
     rows = pair.shape[0]
-    if with_gram:
-        prev = streamed(prev)
-    else:
-        pair = streamed(pair)
-    out_specs = (tiled(), tiled(BW), whole(PADDED))
-    out_shape = (pltpu.HBM((rows, 2 * BW), F32), shape(rows), shape(PADDED))
     return pl.pallas_call(
         rotate_kernel,
         grid=(rows // ROW_TILE,),
+        in_specs=[tiled(), *(tiled(p.shape[1]) for p in prev), whole(stay.shape[0]), whole(sent.shape[0])],
+        out_specs=tiled(),
+        out_shape=pltpu.HBM((rows, 2 * BW), F32),
+        compiler_params=PARAMS,
+    )(streamed(pair), *prev, stay, sent)
+
+
+def rotate_square(pair, prev, stay, sent):
+    rows = pair.shape[0]
+    return pl.pallas_call(
+        rotate_square_kernel,
+        grid=(rows // ROW_TILE,),
         in_specs=[tiled(), tiled(), whole(stay.shape[0]), whole(sent.shape[0])],
-        out_specs=out_specs if with_gram else out_specs[0],
-        out_shape=out_shape if with_gram else out_shape[0],
-        scratch_shapes=[TOTAL] if with_gram else [],
-        compiler_params=PARAMS,
-    )(pair, prev, stay, sent)
-
-
-def join_kernel(prev_ref, cols_ref, passed_ref, out_ref):
-    out_ref[:, :BW] = apply(prev_ref[...], cols_ref[: 2 * BW, :])
-    out_ref[:, BW:] = passed_ref[...]
-
-
-def join_two_kernel(prev_ref, cols_ref, other_ref, other_cols_ref, out_ref):
+        out_specs=[tiled(), tiled(BW), whole(PADDED)],
+        out_shape=[pltpu.HBM((rows, 2 * BW), F32), shape(rows), shape(PADDED)],
+        scratch_shapes=[TOTAL],
+        compiler_params=PARAMS,
+    )(pair, streamed(prev), stay, sent)
+
+
+def join_kernel(prev_ref, cols_ref, other_ref, other_cols_ref, out_ref):
     out_ref[:, :BW] = apply(prev_ref[...], cols_ref[: 2 * BW, :])
     out_ref[:, BW:] = apply(other_ref[...], other_cols_ref[: 2 * BW, :])
 
 
-def join(prev, cols, passed, passed_cols=None):
-    rows = prev.shape[0]
-    if passed_cols is None:
-        prev, passed = streamed(prev), streamed(passed)
-    args = (prev, cols, passed) if passed_cols is None else (prev, cols, passed, passed_cols)
-    return pl.pallas_call(
-        join_kernel if passed_cols is None else join_two_kernel,
+def join(*args):
+    rows = args[0].shape[0]
+    return pl.pallas_call(
+        join_kernel,
         grid=(rows // ROW_TILE,),
         in_specs=[tiled(a.shape[1]) if a.shape[0] == rows else whole(a.shape[0]) for a in args],
         out_specs=tiled(),
-        out_shape=shape(rows, 2 * BW) if passed_cols is None else pltpu.HBM((rows, 2 * BW), F32),
+        out_shape=pltpu.HBM((rows, 2 * BW), F32),
         compiler_params=PARAMS,
     )(*args)
 
@@ -241,6 +279,7 @@
 
 
 def last(pair, left, right):
+    pair = streamed(pair)
     rows = pair.shape[0]
     return pl.pallas_call(
         last_kernel,
@@ -340,18 +379,24 @@
     swapped = jnp.zeros((), bool)
     pair = snapshots
     prev = to_next(pair)
-    product = square(pair)
+    squares = square(pair)
     for stage in range(ROUNDS // 2):
         early, late = 2 * stage, 2 * stage + 1
-        arrived = exchange_all(product)
-        product = product_halves(pair, prev)
+        arrived = exchange_all(squares)
+        if stage == 0:
+            lines = product(pair, prev)
+            prev_parts = [prev]
+        else:
+            kept, lines = stay_product(pair, prev, prev_stay)
+            lines = [lines, *product(pair, passed)]
+            prev_parts = [kept, passed]
         if late + 1 < ROUNDS:
             before = to_next(prev)
         both = pl.pallas_call(
             functools.partial(share_kernel, peers),
             out_shape=shape(PACKED + 4 * BW),
             compiler_params=PARAMS,
-        )(arrived, product)
+        )(arrived, *lines)
         both = exchange_all(both)
         gram, copies = pl.pallas_call(
             functools.partial(split_kernel, peers),
@@ -366,7 +411,7 @@
         swapped = first
         sent = to_next(move)
         labels_b = sent[2 * BW + 1 : 2 * BW + 2]
-        pair = rotate(pair, prev, stay, sent)
+        pair = rotate(pair, prev_parts, stay, sent)
         if late + 1 < ROUNDS:
             prev_stay = to_next(stay)
             sent_before = to_next(sent)
@@ -384,9 +429,8 @@
         sent = to_next(move)
         labels_b = sent[2 * BW + 1 : 2 * BW + 2]
         prev_stay = to_next(stay)
-        pair, came, product = rotate(pair, prev, stay, sent, True)
+        pair, came, squares = rotate_square(pair, prev, stay, sent)
         passed = to_next(came)
-        prev = join(prev, prev_stay, passed)
 
 
 def solution(mesh):

time: 184 us -> 186 us (1.011)
  Pallas kernels: 45 us -> 48.6 us
    pallas_call x4 -> x5, Pallas kernels: 12.1 us -> 19.6 us  [the longest x1 5.25 us: rotate_square(): pl.pallas_call(rotate_square_kernel, grid=(rows // ROW_TILE,), in_specs=[...]
    pallas_call x3 -> x2, Pallas kernels: 13.4 us -> 8.36 us  [rotate(): pl.pallas_call(rotate_kernel, grid=(rows // ROW_TILE,), in_specs=[tiled()...]
  transfers between devices with their start and end apart: 15 -> 15, of which waited for: 8 -> 7; matrix products, arithmetic and copies ran while one was open for 1% -> 1% of each run, Pallas kernels for 17% -> 18%
where the time goes in v4:
time: 186 us; the launch traced here: 185 us
  starting transfers between devices  67.1 us (36%)
  waiting for transfers between devices  66.4 us (36%)
  Pallas kernels  48.6 us (26%)
  between operations  2.29 us (1%)
    all_to_all x6, waiting for transfers between devices, exchange_all(): lax.all_to_all(flat, 'rows', split_axis=0, concat_axis=0, tiled=True)  55.8 us
    all_to_all x6, starting transfers between devices, exchange_all(): lax.all_to_all(flat, 'rows', split_axis=0, concat_axis=0, tiled=True)  49.3 us
    ppermute x9, starting transfers between devices, to_next(): lax.ppermute(value, 'blk', [(i, (i + 1) % peers) for i in range(peers)])  17.8 us
    pallas_call x4, Pallas kernels, columns(): pl.pallas_call(functools.partial(columns_kernel, len(args) > 1), out_shap...  10.8 us
    ppermute x9, waiting for transfers between devices, to_next(): lax.ppermute(value, 'blk', [(i, (i + 1) % peers) for i in range(peers)])  10.6 us
    pallas_call x2, Pallas kernels, rotate(): pl.pallas_call(rotate_kernel, grid=(rows // ROW_TILE,), in_specs=[tiled()...  8.36 us
    pallas_call x1, Pallas kernels, rotate_square(): pl.pallas_call(rotate_square_kernel, grid=(rows // ROW_TILE,), in_specs=[...  5.25 us
    pallas_call x2, Pallas kernels, product(): pl.pallas_call(product_kernel, grid=(left.shape[0] // ROW_TILE,), in_spec...  5.06 us
  transfers between devices with their start and end apart: 15, of which 7 were waited for; matrix products, arithmetic and copies ran while one was open for 1% of the time, Pallas kernels for 18%

profile of v4, /device:TPU:1, one launch (start us, length us, event | category | flops | bytes accessed | tf_op | source)
XLA Modules:
  0.0 185.3 jit_solution(2551342375981020077)
XLA Ops:
  2.6 3.2 %shard_map.37 = f32[512,128]{1,0:T(8,128)} custom-call(f32[2048,256]{1,0:T(8,128)} %pair_ref.1), custom_call_target="tpu_custom_call" | custom-call | tf_op jit(solution)/shard_map/pallas_call | solution.py:148
  5.7 16.3 %all-to-all-start = ((f32[64,1,1024]{2,1,0:T(1,128)}), f32[64,1,1024]{2,1,0:T(1,128)S(1)}, u32[]{:S(2)}, u32[]{:S(2)}) async-start(f32[64,1,1024]{2,1,0:T(1,128)} %bitcast), calls=%async_computation | async-start | bytes 524288 | tf_op jit(solution)/shard_map/all_to_all | solution.py:367
  22.1 3.8 %collective-permute-done.right_ref.refs_0_.prev_ref = f32[2048,256]{1,0:T(8,128)S(1)} collective-permute-done((f32[2048,256]{1,0:T(8,128)}, f32[2048,256]{1,0:T(8,128)S(1)}, u32[]{:S(2)}, u32[]{:S(2)}) %collective-permute-start) | collective-permute-done | bytes 2097184 | tf_op jit(solution)/shard_map/ppermute | solution.py:372
  30.8 5.6 %all-to-all-done = f32[64,1,1024]{2,1,0:T(1,128)S(1)} async-done(((f32[64,1,1024]{2,1,0:T(1,128)}), f32[64,1,1024]{2,1,0:T(1,128)S(1)}, u32[]{:S(2)}, u32[]{:S(2)}) %all-to-all-start) | async-done | bytes 262176 | tf_op jit(solution)/shard_map/all_to_all | solution.py:367
  37.2 10.7 %all-to-all-start.1 = ((f32[64,1,1664]{2,1,0:T(1,128)}), f32[64,1,1664]{2,1,0:T(1,128)S(1)}, u32[]{:S(2)}, u32[]{:S(2)}) async-start(f32[64,1,1664]{2,1,0:T(1,128)} %bitcast.2), calls=%async_computation.1 | async-start | bytes 851968 | tf_op jit(solution)/shard_map/all_to_all | solution.py:367
  50.2 14.0 %all-to-all-done.1 = f32[64,1,1664]{2,1,0:T(1,128)S(1)} async-done(((f32[64,1,1664]{2,1,0:T(1,128)}), f32[64,1,1664]{2,1,0:T(1,128)S(1)}, u32[]{:S(2)}, u32[]{:S(2)}) %all-to-all-start.1) | async-done | bytes 426016 | tf_op jit(solution)/shard_map/all_to_all | solution.py:367
  69.3 5.8 %all-to-all-start.2 = ((f32[64,1,1024]{2,1,0:T(1,128)}), f32[64,1,1024]{2,1,0:T(1,128)S(1)}, u32[]{:S(2)}, u32[]{:S(2)}) async-start(f32[64,1,1024]{2,1,0:T(1,128)} %bitcast.5), calls=%async_computation.2 | async-start | bytes 524288 | tf_op jit(solution)/shard_map/all_to_all | solution.py:367
  77.3 11.9 %all-to-all-done.2 = f32[64,1,1024]{2,1,0:T(1,128)S(1)} async-done(((f32[64,1,1024]{2,1,0:T(1,128)}), f32[64,1,1024]{2,1,0:T(1,128)S(1)}, u32[]{:S(2)}, u32[]{:S(2)}) %all-to-all-start.2) | async-done | bytes 262176 | tf_op jit(solution)/shard_map/all_to_all | solution.py:367
  89.1 2.7 %shard_map.44 = (f32[264,128]{1,0:T(8,128)S(1)}, f32[264,128]{1,0:T(8,128)S(1)}) custom-call(f32[512,128]{1,0:T(8,128)S(1)} %bitcast.34, f32[264,128]{1,0:T(8,128)S(1)} %get-tuple-element.27.refs_1_, f32[264,128]{1,0:T(8,128)S(1)} %collective-permute-done.1.refs_2_, f32[8,128]{1,0:T(8,128)S(1)} %select_select_fusion.2.refs_3_), custom_call_target="tpu_custom_call" | custom-call | tf_op jit(solution)/shard_map/pallas_call | solution.py:358
  93.0 4.2 %shard_map.42.pair_ref = f32[2048,256]{1,0:T(8,128)} custom-call(f32[2048,256]{1,0:T(8,128)} %pair_ref.1, f32[2048,256]{1,0:T(8,128)S(1)} %collective-permute-done.right_ref.refs_0_.prev_ref, f32[264,128]{1,0:T(8,128)S(1)} %get-tuple-element.27.refs_1_, f32[264,128]{1,0:T(8,128)S(1)} %collective-permute-done.1.refs_2_), custom_call_target="tpu_custom_call" | custom-call | tf_op jit(solution)/shard_map/pallas_call | solution.py:235
  97.2 4.4 %shard_map.43.prev_ref = f32[2048,256]{1,0:T(8,128)} custom-call(f32[2048,256]{1,0:T(8,128)S(1)} %collective-permute-done.right_ref.refs_0_.prev_ref, f32[264,128]{1,0:T(8,128)S(1)} %collective-permute-done.2.cols_ref, f32[2048,256]{1,0:T(8,128)} %collective-permute-done.3.other_ref, f32[264,128]{1,0:T(8,128)S(1)} %collective-permute-done.4.other_cols_ref), custom_call_target="tpu_custom_call" | custom-call | tf_op jit(solution)/shard_map/pallas_call | solution.py:265
  101.6 5.3 %shard_map.45 = (f32[2048,256]{1,0:T(8,128)}, f32[2048,128]{1,0:T(8,128)}, f32[512,128]{1,0:T(8,128)}) custom-call(f32[2048,256]{1,0:T(8,128)S(1)} %copy-done, f32[2048,256]{1,0:T(8,128)} %shard_map.43.prev_ref, f32[264,128]{1,0:T(8,128)S(1)} %get-tuple-element.30.stay_ref, f32[264,128]{1,0:T(8,128)S(1)} %collective-permute-done.5.sent_ref), custom_call_target="tpu_custom_call" | custom-call | tf_op jit(solution)/shard_map/pallas_call | solution.py:247
  108.3 4.8 %all-to-all-start.3 = ((f32[64,1,1024]{2,1,0:T(1,128)}), f32[64,1,1024]{2,1,0:T(1,128)S(1)}, u32[]{:S(2)}, u32[]{:S(2)}) async-start(f32[64,1,1024]{2,1,0:T(1,128)} %bitcast.11), calls=%async_computation.3 | async-start | bytes 524288 | tf_op jit(solution)/shard_map/all_to_all | solution.py:367
  115.0 6.8 %collective-permute-done.6.cols_ref = f32[264,128]{1,0:T(8,128)S(1)} collective-permute-done((f32[264,128]{1,0:T(8,128)S(1)}, f32[264,128]{1,0:T(8,128)S(1)}, u32[]{:S(2)}, u32[]{:S(2)}) %collective-permute-start.6) | collective-permute-done | bytes 135200 | tf_op jit(solution)/shard_map/ppermute | solution.py:372
  121.7 5.0 %shard_map.46 = (f32[2048,128]{1,0:T(8,128)S(1)}, f32[256,128]{1,0:T(8,128)S(1)}) custom-call(f32[2048,256]{1,0:T(8,128)} %get-tuple-element.32.left_ref.pair_ref, f32[2048,256]{1,0:T(8,128)} %shard_map.43.prev_ref, f32[264,128]{1,0:T(8,128)S(1)} %collective-permute-done.6.cols_ref), custom_call_target="tpu_custom_call" | custom-call | tf_op jit(solution)/shard_map/pallas_call | solution.py:173
  130.1 7.0 %all-to-all-start.4 = ((f32[64,1,1664]{2,1,0:T(1,128)}), f32[64,1,1664]{2,1,0:T(1,128)S(1)}, u32[]{:S(2)}, u32[]{:S(2)}) async-start(f32[64,1,1664]{2,1,0:T(1,128)} %bitcast.13), calls=%async_computation.4 | async-start | bytes 851968 | tf_op jit(solution)/shard_map/all_to_all | solution.py:367
  137.2 14.1 %all-to-all-done.4 = f32[64,1,1664]{2,1,0:T(1,128)S(1)} async-done(((f32[64,1,1664]{2,1,0:T(1,128)}), f32[64,1,1664]{2,1,0:T(1,128)S(1)}, u32[]{:S(2)}, u32[]{:S(2)}) %all-to-all-start.4) | async-done | bytes 426016 | tf_op jit(solution)/shard_map/all_to_all | solution.py:367
  152.1 2.7 %shard_map.50 = (f32[264,128]{1,0:T(8,128)S(1)}, f32[264,128]{1,0:T(8,128)S(1)}) custom-call(f32[320,128]{1,0:T(8,128)S(1)} %get-tuple-element.37.refs_0_, f32[8,128]{1,0:T(8,128)S(1)} %select_select_fusion.1.refs_1_), custom_call_target="tpu_custom_call" | custom-call | tf_op jit(solution)/shard_map/pallas_call | solution.py:358
  154.8 5.4 %collective-permute-start.8 = (f32[264,128]{1,0:T(8,128)S(1)}, f32[264,128]{1,0:T(8,128)S(1)}, u32[]{:S(2)}, u32[]{:S(2)}) collective-permute-start(f32[264,128]{1,0:T(8,128)S(1)} %get-tuple-element.39), channel_id=1, source_target_pairs={{0,64},{64,128},{128,192},{192,256},{256,320},{320,384},{384,448},... | collective-permute-start | bytes 405512 | tf_op jit(solution)/shard_map/ppermute | solution.py:372
  160.1 4.6 %all-to-all-start.5 = ((f32[64,1,1024]{2,1,0:T(1,128)}), f32[64,1,1024]{2,1,0:T(1,128)S(1)}, u32[]{:S(2)}, u32[]{:S(2)}) async-start(f32[64,1,1024]{2,1,0:T(1,128)} %bitcast.19), calls=%async_computation.5 | async-start | bytes 524288 | tf_op jit(solution)/shard_map/all_to_all | solution.py:367
  164.8 4.2 %shard_map.51.pair_ref = f32[2048,256]{1,0:T(8,128)} custom-call(f32[2048,256]{1,0:T(8,128)} %get-tuple-element.32.left_ref.pair_ref, f32[2048,128]{1,0:T(8,128)S(1)} %get-tuple-element.33.refs_0_, f32[2048,128]{1,0:T(8,128)S(1)} %collective-permute-done.7.right_ref.refs_1_, f32[264,128]{1,0:T(8,128)S(1)} %get-tuple-element.38.refs_2_.refs_1_, ...), custom_call_target="tpu_custom_call" | custom-call | tf_op jit(solution)/shard_map/pallas_call | solution.py:235
  169.0 10.2 %all-to-all-done.5 = f32[64,1,1024]{2,1,0:T(1,128)S(1)} async-done(((f32[64,1,1024]{2,1,0:T(1,128)}), f32[64,1,1024]{2,1,0:T(1,128)S(1)}, u32[]{:S(2)}, u32[]{:S(2)}) %all-to-all-start.5) | async-done | bytes 262176 | tf_op jit(solution)/shard_map/all_to_all | solution.py:367
  179.2 2.7 %shard_map.52 = (f32[264,128]{1,0:T(8,128)S(1)}, f32[264,128]{1,0:T(8,128)S(1)}) custom-call(f32[512,128]{1,0:T(8,128)S(1)} %bitcast.33, f32[264,128]{1,0:T(8,128)S(1)} %get-tuple-element.38.refs_2_.refs_1_, f32[264,128]{1,0:T(8,128)S(1)} %collective-permute-done.8.refs_3_.refs_2_, f32[8,128]{1,0:T(8,128)S(1)} %select_select_fusion.refs_3_), custom_call_target="tpu_custom_call" | custom-call | tf_op jit(solution)/shard_map/pallas_call | solution.py:358
  182.0 3.4 %shard_map.53 = f32[2048,256]{1,0:T(8,128)} custom-call(f32[2048,256]{1,0:T(8,128)} %shard_map.51.pair_ref, f32[264,128]{1,0:T(8,128)S(1)} %get-tuple-element.41.left_ref, f32[264,128]{1,0:T(8,128)S(1)} %get-tuple-element.42.right_ref), custom_call_target="tpu_custom_call" | custom-call | tf_op jit(solution)/shard_map/pallas_call | solution.py:284
  (47 shorter events, 24.5 us)
Async XLA Ops:
  0.0 25.9 %collective-permute-start = (f32[2048,256]{1,0:T(8,128)}, f32[2048,256]{1,0:T(8,128)S(1)}, u32[]{:S(2)}, u32[]{:S(2)}) collective-permute-start(f32[2048,256]{1,0:T(8,128)} %pair_ref.1), channel_id=1, source_target_pairs={{0,64},{64,128},{128,192},{192,256},{256,320},{320,384},{384,448},... | collective-permute-start | bytes 6291464 | tf_op jit(solution)/shard_map/ppermute | solution.py:372
  5.7 30.6 %all-to-all-start = ((f32[64,1,1024]{2,1,0:T(1,128)}), f32[64,1,1024]{2,1,0:T(1,128)S(1)}, u32[]{:S(2)}, u32[]{:S(2)}) async-start(f32[64,1,1024]{2,1,0:T(1,128)} %bitcast), calls=%async_computation | async-start | bytes 524288 | tf_op jit(solution)/shard_map/all_to_all | solution.py:367
  22.1 25.9 %copy-start.1 = (s32[3,1]{0,1:T(1,128)S(1)}, s32[3,1]{0,1:T(1,128)}, u32[]{:S(2)}) copy-start(s32[3,1]{0,1:T(1,128)} %param.5) | copy-start | bytes 40
  22.1 26.6 %copy-start.2 = (s32[256]{0:T(256)S(1)}, s32[256]{0:T(256)}, u32[]{:S(2)}) copy-start(s32[256]{0:T(256)} %param.4) | copy-start | bytes 3076
  25.9 71.3 %collective-permute-start.3 = (f32[2048,256]{1,0:T(8,128)S(1)}, f32[2048,256]{1,0:T(8,128)}, u32[]{:S(2)}, u32[]{:S(2)}) collective-permute-start(f32[2048,256]{1,0:T(8,128)S(1)} %collective-permute-done.right_ref.refs_0_.prev_ref), channel_id=1, source_target_pairs={{0,64},{64,128},{128,192},{192,256},{256,320},{320,384},{384,448},... | collective-permute-start | bytes 6291464 | tf_op jit(solution)/shard_map/ppermute | solution.py:372
  37.2 27.0 %all-to-all-start.1 = ((f32[64,1,1664]{2,1,0:T(1,128)}), f32[64,1,1664]{2,1,0:T(1,128)S(1)}, u32[]{:S(2)}, u32[]{:S(2)}) async-start(f32[64,1,1664]{2,1,0:T(1,128)} %bitcast.2), calls=%async_computation.1 | async-start | bytes 851968 | tf_op jit(solution)/shard_map/all_to_all | solution.py:367
  67.7 8.0 %collective-permute-start.1 = (f32[264,128]{1,0:T(8,128)S(1)}, f32[264,128]{1,0:T(8,128)S(1)}, u32[]{:S(2)}, u32[]{:S(2)}) collective-permute-start(f32[264,128]{1,0:T(8,128)S(1)} %get-tuple-element.28), channel_id=1, source_target_pairs={{0,64},{64,128},{128,192},{192,256},{256,320},{320,384},{384,448},... | collective-permute-start | bytes 405512 | tf_op jit(solution)/shard_map/ppermute | solution.py:372
  69.3 19.8 %all-to-all-start.2 = ((f32[64,1,1024]{2,1,0:T(1,128)}), f32[64,1,1024]{2,1,0:T(1,128)S(1)}, u32[]{:S(2)}, u32[]{:S(2)}) async-start(f32[64,1,1024]{2,1,0:T(1,128)} %bitcast.5), calls=%async_computation.2 | async-start | bytes 524288 | tf_op jit(solution)/shard_map/all_to_all | solution.py:367
  75.2 22.1 %collective-permute-start.2 = (f32[264,128]{1,0:T(8,128)S(1)}, f32[264,128]{1,0:T(8,128)S(1)}, u32[]{:S(2)}, u32[]{:S(2)}) collective-permute-start(f32[264,128]{1,0:T(8,128)S(1)} %get-tuple-element.27.refs_1_), channel_id=1, source_target_pairs={{0,64},{64,128},{128,192},{192,256},{256,320},{320,384},{384,448},... | collective-permute-start | bytes 405512 | tf_op jit(solution)/shard_map/ppermute | solution.py:372
  75.6 21.6 %collective-permute-start.4 = (f32[264,128]{1,0:T(8,128)S(1)}, f32[264,128]{1,0:T(8,128)S(1)}, u32[]{:S(2)}, u32[]{:S(2)}) collective-permute-start(f32[264,128]{1,0:T(8,128)S(1)} %collective-permute-done.1.refs_2_), channel_id=1, source_target_pairs={{0,64},{64,128},{128,192},{192,256},{256,320},{320,384},{384,448},... | collective-permute-start | bytes 405512 | tf_op jit(solution)/shard_map/ppermute | solution.py:372
  91.9 9.7 %collective-permute-start.5 = (f32[264,128]{1,0:T(8,128)S(1)}, f32[264,128]{1,0:T(8,128)S(1)}, u32[]{:S(2)}, u32[]{:S(2)}) collective-permute-start(f32[264,128]{1,0:T(8,128)S(1)} %get-tuple-element.31), channel_id=1, source_target_pairs={{0,64},{64,128},{128,192},{192,256},{256,320},{320,384},{384,448},... | collective-permute-start | bytes 405512 | tf_op jit(solution)/shard_map/ppermute | solution.py:372
  97.2 4.4 %copy-start = (f32[2048,256]{1,0:T(8,128)S(1)}, f32[2048,256]{1,0:T(8,128)}, u32[]{:S(2)}) copy-start(f32[2048,256]{1,0:T(8,128)} %shard_map.42.pair_ref) | copy-start | bytes 6291460
  106.9 19.9 %collective-permute-start.7 = (f32[2048,128]{1,0:T(8,128)}, f32[2048,128]{1,0:T(8,128)S(1)}, u32[]{:S(2)}, u32[]{:S(2)}) collective-permute-start(f32[2048,128]{1,0:T(8,128)} %get-tuple-element.34), channel_id=1, source_target_pairs={{0,64},{64,128},{128,192},{192,256},{256,320},{320,384},{384,448},... | collective-permute-start | bytes 3145736 | tf_op jit(solution)/shard_map/ppermute | solution.py:372
  108.3 20.9 %all-to-all-start.3 = ((f32[64,1,1024]{2,1,0:T(1,128)}), f32[64,1,1024]{2,1,0:T(1,128)S(1)}, u32[]{:S(2)}, u32[]{:S(2)}) async-start(f32[64,1,1024]{2,1,0:T(1,128)} %bitcast.11), calls=%async_computation.3 | async-start | bytes 524288 | tf_op jit(solution)/shard_map/all_to_all | solution.py:367
  113.1 8.6 %collective-permute-start.6 = (f32[264,128]{1,0:T(8,128)S(1)}, f32[264,128]{1,0:T(8,128)S(1)}, u32[]{:S(2)}, u32[]{:S(2)}) collective-permute-start(f32[264,128]{1,0:T(8,128)S(1)} %get-tuple-element.30.stay_ref), channel_id=1, source_target_pairs={{0,64},{64,128},{128,192},{192,256},{256,320},{320,384},{384,448},... | collective-permute-start | bytes 405512 | tf_op jit(solution)/shard_map/ppermute | solution.py:372
  130.1 21.2 %all-to-all-start.4 = ((f32[64,1,1664]{2,1,0:T(1,128)}), f32[64,1,1664]{2,1,0:T(1,128)S(1)}, u32[]{:S(2)}, u32[]{:S(2)}) async-start(f32[64,1,1664]{2,1,0:T(1,128)} %bitcast.13), calls=%async_computation.4 | async-start | bytes 851968 | tf_op jit(solution)/shard_map/all_to_all | solution.py:367
  154.8 10.0 %collective-permute-start.8 = (f32[264,128]{1,0:T(8,128)S(1)}, f32[264,128]{1,0:T(8,128)S(1)}, u32[]{:S(2)}, u32[]{:S(2)}) collective-permute-start(f32[264,128]{1,0:T(8,128)S(1)} %get-tuple-element.39), channel_id=1, source_target_pairs={{0,64},{64,128},{128,192},{192,256},{256,320},{320,384},{384,448},... | collective-permute-start | bytes 405512 | tf_op jit(solution)/shard_map/ppermute | solution.py:372
  160.1 19.1 %all-to-all-start.5 = ((f32[64,1,1024]{2,1,0:T(1,128)}), f32[64,1,1024]{2,1,0:T(1,128)S(1)}, u32[]{:S(2)}, u32[]{:S(2)}) async-start(f32[64,1,1024]{2,1,0:T(1,128)} %bitcast.19), calls=%async_computation.5 | async-start | bytes 524288 | tf_op jit(solution)/shard_map/all_to_all | solution.py:367
